TPU v7x, 256 devices: a whole 4x4x8 slice. The times are simulated.
256 devices in a mesh: gx: 16 (over y_hi, z), gy: 4 (over y_lo, core), gz: 4 (over x).
Axes of the slice: x: 4, y: 4 (y_hi: 2, y_lo: 2; y = y_hi * 2 + y_lo), z: 8, core: 2. Of those that a mesh axis runs over, the one named last changes fastest.
Arguments:
- flow_pops: float32 [19, 128, 32, 512], P(None, 'gx', 'gy', 'gz'), may hold values from 0 to 0.6, as said below
- heat_pops: float32 [7, 128, 32, 512], P(None, 'gx', 'gy', 'gz'), may hold values from -0.2 to 0.2
Outputs:
- flow_out: float32 [19, 128, 32, 512], P(None, 'gx', 'gy', 'gz')
- heat_out: float32 [7, 128, 32, 512], P(None, 'gx', 'gy', 'gz')
- nusselt: float32 [], replicated
Inputs may be any that keep to these rules, and one draw needn't show every extreme that they name: `flow_pops`: positive flow populations.
All inputs are finite; a program needn't handle non-finite values.
Results may differ from a plain program's by a relative error of at most 0.0001.
Values sent between devices are 32-bit elements; how exact they have to be, the bound alone decides.
A program may use at most 64 MiB of HBM per device.

v0:
```python
import functools

import jax
import jax.numpy as jnp
import numpy as np
from jax import lax
from jax.sharding import Mesh
from jax.sharding import PartitionSpec as P

STEPS = 3
GX = ("gx_0", "gx_1")
GY = ("gy_0", "gy_1")
GX_GY_GZ = ("gx_0", "gx_1", "gy_0", "gy_1", "gz")


FLOW_SET = np.array(
    [
        [0, 0, 0],
        [1, 0, 0],
        [-1, 0, 0],
        [0, 1, 0],
        [0, -1, 0],
        [0, 0, 1],
        [0, 0, -1],
        [1, 1, 0],
        [-1, -1, 0],
        [1, -1, 0],
        [-1, 1, 0],
        [1, 0, 1],
        [-1, 0, -1],
        [1, 0, -1],
        [-1, 0, 1],
        [0, 1, 1],
        [0, -1, -1],
        [0, 1, -1],
        [0, -1, 1],
    ]
)
FLOW_WEIGHT = np.array([1.0 / 3.0] + [1.0 / 18.0] * 6 + [1.0 / 36.0] * 12)
D3Q7_QUADRATURE = np.array([0.25] + [0.125] * 6)
LATTICE = np.concatenate([FLOW_SET, FLOW_SET[:7]], axis=0)
WEIGHTS = np.concatenate([FLOW_WEIGHT, D3Q7_QUADRATURE])
OPPOSITE = np.array(
    [[r for r in range(19) if (FLOW_SET[r] == -FLOW_SET[q]).all()][0] for q in range(19)]
    + [19 + [r for r in range(7) if (FLOW_SET[r] == -FLOW_SET[q]).all()][0] for q in range(7)]
)
TAU_FLOW = 0.6
TAU_HEAT = 0.7
GRAVITY_LIFT = 0.01
HOT_WALL = 0.5
COLD_WALL = -0.5
DIFFUSIVITY = (TAU_HEAT - 0.5) / 4.0


def shifted(block, axis, distance):
    devices = range(lax.axis_size(axis))
    route = [((i - distance) % len(devices), i) for i in devices]
    return lax.ppermute(block, axis, route)


def from_behind(value, axis, steps):
    count = lax.axis_size(axis)
    leading, last = (max(0, -steps), min(count, count - steps))
    return lax.ppermute(value, axis, [(source, source + steps) for source in range(leading, last)])


def one_axis_at_a_time(shard, axes):
    return functools.reduce(lax.psum, axes, shard)


def stacked_subarray(values, count):
    return jnp.asarray(values, jnp.float32).reshape(count, 1, 1, 1)


def hydrodynamic_observables(momentum_populations, energy_populations):
    mass_per_site = jnp.sum(momentum_populations, axis=0)
    site_warmth = jnp.sum(energy_populations, axis=0)
    gravity_direction_push = GRAVITY_LIFT * mass_per_site * site_warmth
    speed_xaxis_component = (
        jnp.sum(stacked_subarray(FLOW_SET[:, 0], 19) * momentum_populations, axis=0) / mass_per_site
    )
    speed_yaxis_component = (
        jnp.sum(stacked_subarray(FLOW_SET[:, 1], 19) * momentum_populations, axis=0) / mass_per_site
    )
    speed_zaxis_component = (
        jnp.sum(stacked_subarray(FLOW_SET[:, 2], 19) * momentum_populations, axis=0)
        + 0.5 * gravity_direction_push
    ) / mass_per_site
    return (
        mass_per_site,
        site_warmth,
        gravity_direction_push,
        speed_xaxis_component,
        speed_yaxis_component,
        speed_zaxis_component,
    )


def collide(momentum_populations, energy_populations):
    (
        mass_per_site,
        site_warmth,
        gravity_direction_push,
        speed_xaxis_component,
        speed_yaxis_component,
        speed_zaxis_component,
    ) = hydrodynamic_observables(momentum_populations, energy_populations)
    dir_z = stacked_subarray(FLOW_SET[:, 2], 19)
    projected_onto_link = (
        stacked_subarray(FLOW_SET[:, 0], 19) * speed_xaxis_component
        + stacked_subarray(FLOW_SET[:, 1], 19) * speed_yaxis_component
        + dir_z * speed_zaxis_component
    )
    speed_sq = (
        speed_xaxis_component * speed_xaxis_component
        + speed_yaxis_component * speed_yaxis_component
        + speed_zaxis_component * speed_zaxis_component
    )
    weight = stacked_subarray(FLOW_WEIGHT, 19)
    equil = (
        weight
        * mass_per_site
        * (
            1.0
            + 3.0 * projected_onto_link
            + 4.5 * projected_onto_link * projected_onto_link
            - 1.5 * speed_sq
        )
    )
    source = (
        (1.0 - 0.5 / TAU_FLOW)
        * weight
        * (3.0 * (dir_z - speed_zaxis_component) + 9.0 * projected_onto_link * dir_z)
        * gravity_direction_push
    )
    flow_post = momentum_populations - (momentum_populations - equil) / TAU_FLOW + source
    warmth_rest_distribution = (
        stacked_subarray(D3Q7_QUADRATURE, 7) * site_warmth * (1.0 + 4.0 * projected_onto_link[:7])
    )
    heat_post = energy_populations - (energy_populations - warmth_rest_distribution) / TAU_HEAT
    return jnp.concatenate([flow_post, heat_post], axis=0)


def apply_walls(read, post, is_bottom, is_top):
    result = []
    for member in range(26):
        single = read[member]
        dir_z = int(LATTICE[member, 2])
        if dir_z != 0:
            plane = 0 if dir_z == 1 else single.shape[2] - 1
            flag = is_bottom if dir_z == 1 else is_top
            wall_temp = HOT_WALL if dir_z == 1 else COLD_WALL
            back = post[int(OPPOSITE[member])][:, :, plane]
            if member >= 19:
                back = -back + 2.0 * float(WEIGHTS[member]) * wall_temp
            single = single.at[:, :, plane].set(jnp.where(flag, back, single[:, :, plane]))
        result.append(single)
    return jnp.stack(result)


def local_flux(momentum_populations, energy_populations):
    (
        mass_per_site,
        site_warmth,
        gravity_direction_push,
        speed_xaxis_component,
        speed_yaxis_component,
        speed_zaxis_component,
    ) = hydrodynamic_observables(momentum_populations, energy_populations)
    return jnp.sum(speed_zaxis_component * site_warmth)


def rising(axis_col):
    return np.array([member for member in range(26) if int(LATTICE[member, axis_col]) == 1])


def falling(axis_col):
    return np.array([member for member in range(26) if int(LATTICE[member, axis_col]) == -1])


def last_plane(pops, axis_col):
    length = pops.shape[axis_col + 1]
    return lax.slice_in_dim(pops, length - 1, length, axis=axis_col + 1)[rising(axis_col)]


def first_plane(pops, axis_col):
    return lax.slice_in_dim(pops, 0, 1, axis=axis_col + 1)[falling(axis_col)]


def move_along(pops, axis_col, from_low, from_high):
    result = []
    low_count = 0
    high_count = 0
    length = pops.shape[axis_col + 1]
    for member in range(26):
        single = pops[member]
        moving = int(LATTICE[member, axis_col])
        if moving == 1:
            single = jnp.concatenate(
                [from_low[low_count], lax.slice_in_dim(single, 0, length - 1, axis=axis_col)],
                axis=axis_col,
            )
            low_count += 1
        elif moving == -1:
            single = jnp.concatenate(
                [lax.slice_in_dim(single, 1, length, axis=axis_col), from_high[high_count]],
                axis=axis_col,
            )
            high_count += 1
        result.append(single)
    return jnp.stack(result)


def per_device(flow_pops, heat_pops):
    size_x, size_y, size_z = (flow_pops.shape[1], flow_pops.shape[2], flow_pops.shape[3])
    is_bottom = lax.axis_index("gz") == 0
    is_top = lax.axis_index("gz") == lax.axis_size("gz") - 1
    momentum_populations, energy_populations = (flow_pops, heat_pops)
    for period in range(STEPS):
        post = collide(momentum_populations, energy_populations)
        moved = post
        low_x = shifted(last_plane(moved, 0), GX, 1)
        high_x = shifted(first_plane(moved, 0), GX, -1)
        moved = move_along(moved, 0, low_x, high_x)
        low_y = shifted(last_plane(moved, 1), GY, 1)
        high_y = shifted(first_plane(moved, 1), GY, -1)
        moved = move_along(moved, 1, low_y, high_y)
        low_z = from_behind(last_plane(moved, 2), "gz", 1)
        high_z = from_behind(first_plane(moved, 2), "gz", -1)
        read = move_along(moved, 2, low_z, high_z)
        read = apply_walls(read, post, is_bottom, is_top)
        momentum_populations, energy_populations = (read[:19], read[19:])
    total = one_axis_at_a_time(local_flux(momentum_populations, energy_populations), GX_GY_GZ)
    cells = size_x * size_y * size_z * lax.axis_size(GX) * lax.axis_size(GY) * lax.axis_size("gz")
    height = size_z * lax.axis_size("gz")
    nusselt = 1.0 + height / (DIFFUSIVITY * (HOT_WALL - COLD_WALL)) * total / cells
    return (momentum_populations, energy_populations, nusselt)


def solution(mesh):
    torus = Mesh(
        mesh.devices.reshape(2, 8, 2, 2, mesh.shape["gz"]), ("gx_0", "gx_1", "gy_0", "gy_1", "gz")
    )
    return jax.shard_map(
        per_device,
        mesh=torus,
        in_specs=(P(None, GX, GY, "gz"), P(None, GX, GY, "gz")),
        out_specs=(P(None, GX, GY, "gz"), P(None, GX, GY, "gz"), P()),
        check_vma=False,
    )
```

profile of v0, /device:TPU:1, one launch (start us, length us, event | category | flops | bytes accessed | tf_op | source)
XLA Modules:
  0.0 234.9 jit_solution(3908384848769976948)
XLA Ops:
  1.3 1.0 reduce_sum.665
  2.4 1.3 multiply_reduce_fusion.9
  6.5 2.5 %collective-permute-start = (f32[6,1,8,128]{3,2,1,0:T(8,128)S(1)}, f32[6,1,8,128]{3,2,1,0:T(8,128)S(1)}, u32[]{:S(2)}, u32[]{:S(2)}) collective-permute-start(f32[6,1,8,128]{3,2,1,0:T(8,128)S(1)} %bitcast.1389), channel_id=1, source_target_pairs={{240,0},{0,16},{16,32},{32,48},{48,64},{64,80},{80,96},{96,112},{1... | collective-permute-start | bytes 73736 | tf_op jit(solution)/shard_map/ppermute | solution.py:58
  9.6 7.2 %collective-permute-start.1 = (f32[6,1,8,128]{3,2,1,0:T(8,128)S(1)}, f32[6,1,8,128]{3,2,1,0:T(8,128)S(1)}, u32[]{:S(2)}, u32[]{:S(2)}) collective-permute-start(f32[6,1,8,128]{3,2,1,0:T(8,128)S(1)} %bitcast.1388), channel_id=1, source_target_pairs={{16,0},{32,16},{48,32},{64,48},{80,64},{96,80},{112,96},{128,112},... | collective-permute-start | bytes 73736 | tf_op jit(solution)/shard_map/ppermute | solution.py:58
  25.1 1.3 collective-permute-start.2
  28.6 1.7 collective-permute-done.3
  33.1 0.7 fusion.98
  37.3 1.3 copy.1081
  39.7 3.1 %collective-permute-start.4 = (f32[6,8,8,1]{3,2,1,0:T(8,128)S(1)}, f32[6,8,8,1]{3,2,1,0:T(8,128)S(1)}, u32[]{:S(2)}, u32[]{:S(2)}) collective-permute-start(f32[6,8,8,1]{3,2,1,0:T(8,128)S(1)} %copy.971), channel_id=1, source_target_pairs={{0,1},{1,2},{2,3},{4,5},{5,6},{6,7},{8,9},{9,10},{10,11},{12,13},{... | collective-permute-start | bytes 4616 | tf_op jit(solution)/shard_map/ppermute | solution.py:64
  42.9 1.3 copy.1082
  45.2 1.3 collective-permute-start.5
  46.8 0.7 copy-done.42
  47.7 5.3 %collective-permute-done.5 = f32[6,8,8,1]{3,2,1,0:T(8,128)S(1)} collective-permute-done((f32[6,8,8,1]{3,2,1,0:T(8,128)S(1)}, f32[6,8,8,1]{3,2,1,0:T(8,128)S(1)}, u32[]{:S(2)}, u32[]{:S(2)}) %collective-permute-start.5) | collective-permute-done | bytes 1568 | tf_op jit(solution)/shard_map/ppermute | solution.py:64
  54.5 0.7 copy-done.17
  55.9 0.7 copy-done.15
  56.7 0.7 copy-done.142
  57.6 0.7 copy-done.141
  59.0 0.7 copy-done.140
  60.5 0.7 copy-done.139
  61.4 0.7 copy-done.136
  62.3 0.7 copy-done.131
  63.7 0.7 copy-done.130
  74.7 5.1 %collective-permute-start.7 = (f32[6,1,8,128]{3,2,1,0:T(8,128)S(1)}, f32[6,1,8,128]{3,2,1,0:T(8,128)S(1)}, u32[]{:S(2)}, u32[]{:S(2)}) collective-permute-start(f32[6,1,8,128]{3,2,1,0:T(8,128)S(1)} %bitcast.1390), channel_id=1, source_target_pairs={{16,0},{32,16},{48,32},{64,48},{80,64},{96,80},{112,96},{128,112},... | collective-permute-start | bytes 73736 | tf_op jit(solution)/shard_map/ppermute | solution.py:58
  86.1 3.0 %collective-permute-start.8 = (f32[6,8,1,128]{3,2,1,0:T(1,128)S(1)}, f32[6,8,1,128]{3,2,1,0:T(1,128)S(1)}, u32[]{:S(2)}, u32[]{:S(2)}) collective-permute-start(f32[6,8,1,128]{3,2,1,0:T(1,128)S(1)} %bitcast.1399), channel_id=1, source_target_pairs={{12,0},{0,4},{4,8},{8,12},{13,1},{1,5},{5,9},{9,13},{14,2},{2,6},{... | collective-permute-start | bytes 73736 | tf_op jit(solution)/shard_map/ppermute | solution.py:58
  91.8 2.0 collective-permute-done.9
  96.6 0.7 fusion.82
  100.8 1.3 copy.1083
  103.2 3.1 %collective-permute-start.10 = (f32[6,8,8,1]{3,2,1,0:T(8,128)S(1)}, f32[6,8,8,1]{3,2,1,0:T(8,128)S(1)}, u32[]{:S(2)}, u32[]{:S(2)}) collective-permute-start(f32[6,8,8,1]{3,2,1,0:T(8,128)S(1)} %copy.1013), channel_id=1, source_target_pairs={{0,1},{1,2},{2,3},{4,5},{5,6},{6,7},{8,9},{9,10},{10,11},{12,13},{... | collective-permute-start | bytes 4616 | tf_op jit(solution)/shard_map/ppermute | solution.py:64
  106.4 1.3 copy.1084
  108.7 1.3 collective-permute-start.11
  111.5 5.7 %collective-permute-done.11 = f32[6,8,8,1]{3,2,1,0:T(8,128)S(1)} collective-permute-done((f32[6,8,8,1]{3,2,1,0:T(8,128)S(1)}, f32[6,8,8,1]{3,2,1,0:T(8,128)S(1)}, u32[]{:S(2)}, u32[]{:S(2)}) %collective-permute-start.11) | collective-permute-done | bytes 1568 | tf_op jit(solution)/shard_map/ppermute | solution.py:64
  119.3 0.7 copy-done.11
  120.0 0.7 copy-done.13
  120.8 0.7 copy-done.127
  121.7 0.7 copy-done.125
  123.2 0.7 copy-done.123
  124.6 0.7 copy-done.128
  125.5 0.7 copy-done.137
  126.4 0.7 copy-done.134
  127.9 0.7 copy-done.132
  135.0 0.7 copy-done.23
  138.1 5.2 %collective-permute-start.13 = (f32[6,1,8,128]{3,2,1,0:T(8,128)S(1)}, f32[6,1,8,128]{3,2,1,0:T(8,128)S(1)}, u32[]{:S(2)}, u32[]{:S(2)}) collective-permute-start(f32[6,1,8,128]{3,2,1,0:T(8,128)S(1)} %bitcast.1391), channel_id=1, source_target_pairs={{16,0},{32,16},{48,32},{64,48},{80,64},{96,80},{112,96},{128,112},... | collective-permute-start | bytes 73736 | tf_op jit(solution)/shard_map/ppermute | solution.py:58
  148.4 2.1 collective-permute-start.14
  153.2 2.0 collective-permute-done.15
  160.4 1.3 copy.1085
  162.8 2.8 %collective-permute-start.16 = (f32[6,8,8,1]{3,2,1,0:T(8,128)S(1)}, f32[6,8,8,1]{3,2,1,0:T(8,128)S(1)}, u32[]{:S(2)}, u32[]{:S(2)}) collective-permute-start(f32[6,8,8,1]{3,2,1,0:T(8,128)S(1)} %copy.1053), channel_id=1, source_target_pairs={{0,1},{1,2},{2,3},{4,5},{5,6},{6,7},{8,9},{9,10},{10,11},{12,13},{... | collective-permute-start | bytes 4616 | tf_op jit(solution)/shard_map/ppermute | solution.py:64
  165.7 1.3 copy.1086
  168.0 1.3 collective-permute-start.17
  171.1 5.7 %collective-permute-done.17 = f32[6,8,8,1]{3,2,1,0:T(8,128)S(1)} collective-permute-done((f32[6,8,8,1]{3,2,1,0:T(8,128)S(1)}, f32[6,8,8,1]{3,2,1,0:T(8,128)S(1)}, u32[]{:S(2)}, u32[]{:S(2)}) %collective-permute-start.17) | collective-permute-done | bytes 1568 | tf_op jit(solution)/shard_map/ppermute | solution.py:64
  179.0 0.7 copy-done.7
  179.7 0.7 copy-done.9
  180.5 0.7 copy-done.126
  181.4 0.7 copy-done.124
  182.8 0.7 copy-done.122
  184.3 0.7 copy-done.129
  185.2 0.7 copy-done.138
  186.1 0.7 copy-done.135
  187.5 0.7 copy-done.133
  191.0 0.7 multiply_reduce_fusion.10
  191.7 5.9 %psum.35 = f32[]{:T(128)} all-reduce(f32[]{:T(128)} %multiply_reduce_fusion.10), channel_id=1, replica_groups=mesh['gx_0'=2,'gx_1'=8,'gy_0'=2,'gy_1'=2,'gz'=4] {'gx_0'}, use_global_device_ids=true, to_apply=%region_13.14 | all-reduce | flops 1 | bytes 8 | tf_op jit(solution)/shard_map/psum | solution.py:68
  197.6 13.9 %psum.36 = f32[]{:T(128)} all-reduce(f32[]{:T(128)} %psum.35), channel_id=1, replica_groups=mesh['gx_0'=2,'gx_1'=8,'gy_0'=2,'gy_1'=2,'gz'=4] {'gx_1'}, use_global_device_ids=true, to_apply=%region_14.15 | all-reduce | flops 1 | bytes 8 | tf_op jit(solution)/shard_map/psum | solution.py:68
  211.5 4.7 %psum.37 = f32[]{:T(128)} all-reduce(f32[]{:T(128)} %psum.36), channel_id=1, replica_groups=mesh['gx_0'=2,'gx_1'=8,'gy_0'=2,'gy_1'=2,'gz'=4] {'gy_0'}, use_global_device_ids=true, to_apply=%region_15.16 | all-reduce | flops 1 | bytes 8 | tf_op jit(solution)/shard_map/psum | solution.py:68
  216.8 8.9 %psum.38 = f32[]{:T(128)} all-reduce(f32[]{:T(128)} %psum.37), channel_id=1, replica_groups=mesh['gx_0'=2,'gx_1'=8,'gy_0'=2,'gy_1'=2,'gz'=4] {'gy_1'}, use_global_device_ids=true, to_apply=%region_16.17 | all-reduce | flops 1 | bytes 8 | tf_op jit(solution)/shard_map/psum | solution.py:68
  226.4 6.7 %psum.39 = f32[]{:T(128)} all-reduce(f32[]{:T(128)} %psum.38), channel_id=1, replica_groups=mesh['gx_0'=2,'gx_1'=8,'gy_0'=2,'gy_1'=2,'gz'=4] {'gz'}, use_global_device_ids=true, to_apply=%region_17.18 | all-reduce | flops 1 | bytes 8 | tf_op jit(solution)/shard_map/psum | solution.py:68
  (837 shorter events, 93.2 us)
Async XLA Ops:
  6.5 13.8 %collective-permute-start = (f32[6,1,8,128]{3,2,1,0:T(8,128)S(1)}, f32[6,1,8,128]{3,2,1,0:T(8,128)S(1)}, u32[]{:S(2)}, u32[]{:S(2)}) collective-permute-start(f32[6,1,8,128]{3,2,1,0:T(8,128)S(1)} %bitcast.1389), channel_id=1, source_target_pairs={{240,0},{0,16},{16,32},{32,48},{48,64},{64,80},{80,96},{96,112},{1... | collective-permute-start | bytes 73736 | tf_op jit(solution)/shard_map/ppermute | solution.py:58
  9.6 11.9 %collective-permute-start.1 = (f32[6,1,8,128]{3,2,1,0:T(8,128)S(1)}, f32[6,1,8,128]{3,2,1,0:T(8,128)S(1)}, u32[]{:S(2)}, u32[]{:S(2)}) collective-permute-start(f32[6,1,8,128]{3,2,1,0:T(8,128)S(1)} %bitcast.1388), channel_id=1, source_target_pairs={{16,0},{32,16},{48,32},{64,48},{80,64},{96,80},{112,96},{128,112},... | collective-permute-start | bytes 73736 | tf_op jit(solution)/shard_map/ppermute | solution.py:58
  17.5 10.5 %copy-start.38 = (f32[8,8,128]{2,1,0:T(8,128)}, f32[8,8,128]{2,1,0:T(8,128)S(1)}, u32[]{:S(2)}) copy-start(f32[8,8,128]{2,1,0:T(8,128)S(1)} %get-tuple-element.547) | copy-start | bytes 98308
  18.2 17.5 %copy-start.18 = (f32[7,8,128]{2,1,0:T(8,128)}, f32[7,8,128]{2,1,0:T(8,128)S(1)}, u32[]{:S(2)}) copy-start(f32[7,8,128]{2,1,0:T(8,128)S(1)} %get-tuple-element.584) | copy-start | bytes 86020
  18.2 17.5 %copy-start.20 = (f32[7,8,128]{2,1,0:T(8,128)}, f32[7,8,128]{2,1,0:T(8,128)S(1)}, u32[]{:S(2)}) copy-start(f32[7,8,128]{2,1,0:T(8,128)S(1)} %get-tuple-element.585) | copy-start | bytes 86020
  18.9 5.6 %copy-start.220 = (s32[1024]{0:T(1024)}, s32[1024]{0:T(1024)S(1)}, u32[]{:S(2)}) copy-start(s32[1024]{0:T(1024)S(1)} %get-tuple-element.817) | copy-start | bytes 12292
  18.9 7.5 %copy-start.219 = (s32[1024]{0:T(1024)}, s32[1024]{0:T(1024)S(1)}, u32[]{:S(2)}) copy-start(s32[1024]{0:T(1024)S(1)} %get-tuple-element.816) | copy-start | bytes 12292
  19.5 11.4 %copy-start.51 = (f32[8,7,128]{2,1,0:T(8,128)}, f32[8,7,128]{2,1,0:T(8,128)S(1)}, u32[]{:S(2)}) copy-start(f32[8,7,128]{2,1,0:T(8,128)S(1)} %slice.2411) | copy-start | bytes 86020
  19.6 14.2 %copy-start.77 = (f32[8,7,128]{2,1,0:T(8,128)}, f32[8,7,128]{2,1,0:T(8,128)S(1)}, u32[]{:S(2)}) copy-start(f32[8,7,128]{2,1,0:T(8,128)S(1)} %slice.2437) | copy-start | bytes 86020
  22.9 8.7 %copy-start.16 = (f32[8,7,128]{2,1,0:T(8,128)}, f32[8,7,128]{2,1,0:T(8,128)S(1)}, u32[]{:S(2)}) copy-start(f32[8,7,128]{2,1,0:T(8,128)S(1)} %get-tuple-element.813) | copy-start | bytes 86020
  22.9 8.7 %copy-start.14 = (f32[8,7,128]{2,1,0:T(8,128)}, f32[8,7,128]{2,1,0:T(8,128)S(1)}, u32[]{:S(2)}) copy-start(f32[8,7,128]{2,1,0:T(8,128)S(1)} %get-tuple-element.812) | copy-start | bytes 86020
  25.1 2.3 collective-permute-start.2
  26.9 3.3 %collective-permute-start.3 = (f32[6,8,1,128]{3,2,1,0:T(1,128)S(1)}, f32[6,8,1,128]{3,2,1,0:T(1,128)S(1)}, u32[]{:S(2)}, u32[]{:S(2)}) collective-permute-start(f32[6,8,1,128]{3,2,1,0:T(1,128)S(1)} %bitcast.1392), channel_id=1, source_target_pairs={{4,0},{8,4},{12,8},{0,12},{5,1},{9,5},{13,9},{1,13},{6,2},{10,6},{... | collective-permute-start | bytes 73736 | tf_op jit(solution)/shard_map/ppermute | solution.py:58
  27.9 7.8 %copy-start.173 = (f32[8,1,128]{2,1,0:T(1,128)}, f32[8,1,128]{2,1,0:T(1,128)S(1)}, u32[]{:S(2)}) copy-start(f32[8,1,128]{2,1,0:T(1,128)S(1)} %get-tuple-element.795) | copy-start | bytes 12292
  39.7 7.0 %collective-permute-start.4 = (f32[6,8,8,1]{3,2,1,0:T(8,128)S(1)}, f32[6,8,8,1]{3,2,1,0:T(8,128)S(1)}, u32[]{:S(2)}, u32[]{:S(2)}) collective-permute-start(f32[6,8,8,1]{3,2,1,0:T(8,128)S(1)} %copy.971), channel_id=1, source_target_pairs={{0,1},{1,2},{2,3},{4,5},{5,6},{6,7},{8,9},{9,10},{10,11},{12,13},{... | collective-permute-start | bytes 4616 | tf_op jit(solution)/shard_map/ppermute | solution.py:64
  45.2 7.8 %collective-permute-start.5 = (f32[6,8,8,1]{3,2,1,0:T(8,128)S(1)}, f32[6,8,8,1]{3,2,1,0:T(8,128)S(1)}, u32[]{:S(2)}, u32[]{:S(2)}) collective-permute-start(f32[6,8,8,1]{3,2,1,0:T(8,128)S(1)} %copy.976), channel_id=1, source_target_pairs={{1,0},{2,1},{3,2},{5,4},{6,5},{7,6},{9,8},{10,9},{11,10},{13,12},{... | collective-permute-start | bytes 4616 | tf_op jit(solution)/shard_map/ppermute | solution.py:64
  47.5 5.5 %copy-start.107 = (f32[8,8,128]{2,1,0:T(8,128)S(1)}, f32[8,8,128]{2,1,0:T(8,128)}, u32[]{:S(2)}) copy-start(f32[8,8,128]{2,1,0:T(8,128)} %get-tuple-element.537) | copy-start | bytes 98308
  47.5 5.5 %copy-start.108 = (f32[8,8,128]{2,1,0:T(8,128)S(1)}, f32[8,8,128]{2,1,0:T(8,128)}, u32[]{:S(2)}) copy-start(f32[8,8,128]{2,1,0:T(8,128)} %get-tuple-element.538) | copy-start | bytes 98308
  70.7 9.1 %copy-start.69 = (f32[8,8,128]{2,1,0:T(8,128)}, f32[8,8,128]{2,1,0:T(8,128)S(1)}, u32[]{:S(2)}) copy-start(f32[8,8,128]{2,1,0:T(8,128)S(1)} %get-tuple-element.520) | copy-start | bytes 98308
  70.7 9.1 %copy-start.59 = (f32[8,8,128]{2,1,0:T(8,128)}, f32[8,8,128]{2,1,0:T(8,128)S(1)}, u32[]{:S(2)}) copy-start(f32[8,8,128]{2,1,0:T(8,128)S(1)} %get-tuple-element.518) | copy-start | bytes 98308
  70.7 9.2 %copy-start.67 = (f32[8,8,128]{2,1,0:T(8,128)}, f32[8,8,128]{2,1,0:T(8,128)S(1)}, u32[]{:S(2)}) copy-start(f32[8,8,128]{2,1,0:T(8,128)S(1)} %get-tuple-element.516) | copy-start | bytes 98308
  70.7 20.4 %copy-start.36 = (f32[8,8,128]{2,1,0:T(8,128)}, f32[8,8,128]{2,1,0:T(8,128)S(1)}, u32[]{:S(2)}) copy-start(f32[8,8,128]{2,1,0:T(8,128)S(1)} %get-tuple-element.523) | copy-start | bytes 98308
  71.6 9.6 %copy-start.97 = (f32[7,8,128]{2,1,0:T(8,128)}, f32[7,8,128]{2,1,0:T(8,128)S(1)}, u32[]{:S(2)}) copy-start(f32[7,8,128]{2,1,0:T(8,128)S(1)} %get-tuple-element.534) | copy-start | bytes 86020
  71.6 10.8 %copy-start.95 = (f32[7,8,128]{2,1,0:T(8,128)}, f32[7,8,128]{2,1,0:T(8,128)S(1)}, u32[]{:S(2)}) copy-start(f32[7,8,128]{2,1,0:T(8,128)S(1)} %get-tuple-element.533) | copy-start | bytes 86020
  73.1 7.5 %collective-permute-start.6 = (f32[6,1,8,128]{3,2,1,0:T(8,128)S(1)}, f32[6,1,8,128]{3,2,1,0:T(8,128)S(1)}, u32[]{:S(2)}, u32[]{:S(2)}) collective-permute-start(f32[6,1,8,128]{3,2,1,0:T(8,128)S(1)} %bitcast.1395), channel_id=1, source_target_pairs={{240,0},{0,16},{16,32},{32,48},{48,64},{64,80},{80,96},{96,112},{1... | collective-permute-start | bytes 73736 | tf_op jit(solution)/shard_map/ppermute | solution.py:58
  74.0 25.2 %copy-start.22 = (f32[7,8,128]{2,1,0:T(8,128)}, f32[7,8,128]{2,1,0:T(8,128)S(1)}, u32[]{:S(2)}) copy-start(f32[7,8,128]{2,1,0:T(8,128)S(1)} %get-tuple-element.574) | copy-start | bytes 86020
  74.0 25.2 %copy-start.24 = (f32[7,8,128]{2,1,0:T(8,128)}, f32[7,8,128]{2,1,0:T(8,128)S(1)}, u32[]{:S(2)}) copy-start(f32[7,8,128]{2,1,0:T(8,128)S(1)} %get-tuple-element.575) | copy-start | bytes 86020
  74.7 7.1 %collective-permute-start.7 = (f32[6,1,8,128]{3,2,1,0:T(8,128)S(1)}, f32[6,1,8,128]{3,2,1,0:T(8,128)S(1)}, u32[]{:S(2)}, u32[]{:S(2)}) collective-permute-start(f32[6,1,8,128]{3,2,1,0:T(8,128)S(1)} %bitcast.1390), channel_id=1, source_target_pairs={{16,0},{32,16},{48,32},{64,48},{80,64},{96,80},{112,96},{128,112},... | collective-permute-start | bytes 73736 | tf_op jit(solution)/shard_map/ppermute | solution.py:58
  79.9 14.6 %copy-start.55 = (f32[8,7,128]{2,1,0:T(8,128)}, f32[8,7,128]{2,1,0:T(8,128)S(1)}, u32[]{:S(2)}) copy-start(f32[8,7,128]{2,1,0:T(8,128)S(1)} %slice.2535) | copy-start | bytes 86020
  79.9 17.4 %copy-start.79 = (f32[8,7,128]{2,1,0:T(8,128)}, f32[8,7,128]{2,1,0:T(8,128)S(1)}, u32[]{:S(2)}) copy-start(f32[8,7,128]{2,1,0:T(8,128)S(1)} %slice.2561) | copy-start | bytes 86020
  83.2 11.9 %copy-start.10 = (f32[8,7,128]{2,1,0:T(8,128)}, f32[8,7,128]{2,1,0:T(8,128)S(1)}, u32[]{:S(2)}) copy-start(f32[8,7,128]{2,1,0:T(8,128)S(1)} %fusion.52) | copy-start | bytes 86020
  83.2 11.9 %copy-start.12 = (f32[8,7,128]{2,1,0:T(8,128)}, f32[8,7,128]{2,1,0:T(8,128)S(1)}, u32[]{:S(2)}) copy-start(f32[8,7,128]{2,1,0:T(8,128)S(1)} %fusion.51) | copy-start | bytes 86020
  86.1 4.4 %collective-permute-start.8 = (f32[6,8,1,128]{3,2,1,0:T(1,128)S(1)}, f32[6,8,1,128]{3,2,1,0:T(1,128)S(1)}, u32[]{:S(2)}, u32[]{:S(2)}) collective-permute-start(f32[6,8,1,128]{3,2,1,0:T(1,128)S(1)} %bitcast.1399), channel_id=1, source_target_pairs={{12,0},{0,4},{4,8},{8,12},{13,1},{1,5},{5,9},{9,13},{14,2},{2,6},{... | collective-permute-start | bytes 73736 | tf_op jit(solution)/shard_map/ppermute | solution.py:58
  90.5 3.3 %collective-permute-start.9 = (f32[6,8,1,128]{3,2,1,0:T(1,128)S(1)}, f32[6,8,1,128]{3,2,1,0:T(1,128)S(1)}, u32[]{:S(2)}, u32[]{:S(2)}) collective-permute-start(f32[6,8,1,128]{3,2,1,0:T(1,128)S(1)} %bitcast.1393), channel_id=1, source_target_pairs={{4,0},{8,4},{12,8},{0,12},{5,1},{9,5},{13,9},{1,13},{6,2},{10,6},{... | collective-permute-start | bytes 73736 | tf_op jit(solution)/shard_map/ppermute | solution.py:58
  91.2 8.1 %copy-start.171 = (f32[8,1,128]{2,1,0:T(1,128)}, f32[8,1,128]{2,1,0:T(1,128)S(1)}, u32[]{:S(2)}) copy-start(f32[8,1,128]{2,1,0:T(1,128)S(1)} %get-tuple-element.767) | copy-start | bytes 12292
  103.2 7.3 %collective-permute-start.10 = (f32[6,8,8,1]{3,2,1,0:T(8,128)S(1)}, f32[6,8,8,1]{3,2,1,0:T(8,128)S(1)}, u32[]{:S(2)}, u32[]{:S(2)}) collective-permute-start(f32[6,8,8,1]{3,2,1,0:T(8,128)S(1)} %copy.1013), channel_id=1, source_target_pairs={{0,1},{1,2},{2,3},{4,5},{5,6},{6,7},{8,9},{9,10},{10,11},{12,13},{... | collective-permute-start | bytes 4616 | tf_op jit(solution)/shard_map/ppermute | solution.py:64
  108.7 8.4 %collective-permute-start.11 = (f32[6,8,8,1]{3,2,1,0:T(8,128)S(1)}, f32[6,8,8,1]{3,2,1,0:T(8,128)S(1)}, u32[]{:S(2)}, u32[]{:S(2)}) collective-permute-start(f32[6,8,8,1]{3,2,1,0:T(8,128)S(1)} %copy.1018), channel_id=1, source_target_pairs={{1,0},{2,1},{3,2},{5,4},{6,5},{7,6},{9,8},{10,9},{11,10},{13,12},{... | collective-permute-start | bytes 4616 | tf_op jit(solution)/shard_map/ppermute | solution.py:64
  110.6 6.6 %copy-start.105 = (f32[8,8,128]{2,1,0:T(8,128)S(1)}, f32[8,8,128]{2,1,0:T(8,128)}, u32[]{:S(2)}) copy-start(f32[8,8,128]{2,1,0:T(8,128)} %get-tuple-element.513) | copy-start | bytes 98308
  110.6 6.5 %copy-start.106 = (f32[8,8,128]{2,1,0:T(8,128)S(1)}, f32[8,8,128]{2,1,0:T(8,128)}, u32[]{:S(2)}) copy-start(f32[8,8,128]{2,1,0:T(8,128)} %get-tuple-element.514) | copy-start | bytes 98308
  111.4 5.7 %copy-start.60 = (f32[8,8,128]{2,1,0:T(8,128)S(1)}, f32[8,8,128]{2,1,0:T(8,128)}, u32[]{:S(2)}) copy-start(f32[8,8,128]{2,1,0:T(8,128)} %copy-done.59) | copy-start | bytes 98308
  111.4 5.7 %copy-start.86 = (f32[8,8,128]{2,1,0:T(8,128)S(1)}, f32[8,8,128]{2,1,0:T(8,128)}, u32[]{:S(2)}) copy-start(f32[8,8,128]{2,1,0:T(8,128)} %get-tuple-element.570) | copy-start | bytes 98308
  134.9 8.4 %copy-start.65 = (f32[8,8,128]{2,1,0:T(8,128)}, f32[8,8,128]{2,1,0:T(8,128)S(1)}, u32[]{:S(2)}) copy-start(f32[8,8,128]{2,1,0:T(8,128)S(1)} %get-tuple-element.496) | copy-start | bytes 98308
  134.9 8.4 %copy-start.57 = (f32[8,8,128]{2,1,0:T(8,128)}, f32[8,8,128]{2,1,0:T(8,128)S(1)}, u32[]{:S(2)}) copy-start(f32[8,8,128]{2,1,0:T(8,128)S(1)} %get-tuple-element.494) | copy-start | bytes 98308
  134.9 8.4 %copy-start.63 = (f32[8,8,128]{2,1,0:T(8,128)}, f32[8,8,128]{2,1,0:T(8,128)S(1)}, u32[]{:S(2)}) copy-start(f32[8,8,128]{2,1,0:T(8,128)S(1)} %get-tuple-element.492) | copy-start | bytes 98308
  134.9 17.1 %copy-start.34 = (f32[8,8,128]{2,1,0:T(8,128)}, f32[8,8,128]{2,1,0:T(8,128)S(1)}, u32[]{:S(2)}) copy-start(f32[8,8,128]{2,1,0:T(8,128)S(1)} %get-tuple-element.499) | copy-start | bytes 98308
  135.8 8.3 %copy-start.93 = (f32[7,8,128]{2,1,0:T(8,128)}, f32[7,8,128]{2,1,0:T(8,128)S(1)}, u32[]{:S(2)}) copy-start(f32[7,8,128]{2,1,0:T(8,128)S(1)} %get-tuple-element.510) | copy-start | bytes 86020
  135.8 8.9 %copy-start.91 = (f32[7,8,128]{2,1,0:T(8,128)}, f32[7,8,128]{2,1,0:T(8,128)S(1)}, u32[]{:S(2)}) copy-start(f32[7,8,128]{2,1,0:T(8,128)S(1)} %get-tuple-element.509) | copy-start | bytes 86020
  137.3 6.7 %collective-permute-start.12 = (f32[6,1,8,128]{3,2,1,0:T(8,128)S(1)}, f32[6,1,8,128]{3,2,1,0:T(8,128)S(1)}, u32[]{:S(2)}, u32[]{:S(2)}) collective-permute-start(f32[6,1,8,128]{3,2,1,0:T(8,128)S(1)} %bitcast.1396), channel_id=1, source_target_pairs={{240,0},{0,16},{16,32},{32,48},{48,64},{64,80},{80,96},{96,112},{1... | collective-permute-start | bytes 73736 | tf_op jit(solution)/shard_map/ppermute | solution.py:58
  137.4 21.4 %copy-start.28 = (f32[7,8,128]{2,1,0:T(8,128)}, f32[7,8,128]{2,1,0:T(8,128)S(1)}, u32[]{:S(2)}) copy-start(f32[7,8,128]{2,1,0:T(8,128)S(1)} %get-tuple-element.566) | copy-start | bytes 86020
  137.4 21.4 %copy-start.26 = (f32[7,8,128]{2,1,0:T(8,128)}, f32[7,8,128]{2,1,0:T(8,128)S(1)}, u32[]{:S(2)}) copy-start(f32[7,8,128]{2,1,0:T(8,128)S(1)} %get-tuple-element.565) | copy-start | bytes 86020
  138.1 6.6 %collective-permute-start.13 = (f32[6,1,8,128]{3,2,1,0:T(8,128)S(1)}, f32[6,1,8,128]{3,2,1,0:T(8,128)S(1)}, u32[]{:S(2)}, u32[]{:S(2)}) collective-permute-start(f32[6,1,8,128]{3,2,1,0:T(8,128)S(1)} %bitcast.1391), channel_id=1, source_target_pairs={{16,0},{32,16},{48,32},{64,48},{80,64},{96,80},{112,96},{128,112},... | collective-permute-start | bytes 73736 | tf_op jit(solution)/shard_map/ppermute | solution.py:58
  143.3 12.0 %copy-start.53 = (f32[8,7,128]{2,1,0:T(8,128)}, f32[8,7,128]{2,1,0:T(8,128)S(1)}, u32[]{:S(2)}) copy-start(f32[8,7,128]{2,1,0:T(8,128)S(1)} %slice.2659) | copy-start | bytes 86020
  143.3 14.8 %copy-start.81 = (f32[8,7,128]{2,1,0:T(8,128)}, f32[8,7,128]{2,1,0:T(8,128)S(1)}, u32[]{:S(2)}) copy-start(f32[8,7,128]{2,1,0:T(8,128)S(1)} %slice.2685) | copy-start | bytes 86020
  145.5 10.4 %copy-start.6 = (f32[8,7,128]{2,1,0:T(8,128)}, f32[8,7,128]{2,1,0:T(8,128)S(1)}, u32[]{:S(2)}) copy-start(f32[8,7,128]{2,1,0:T(8,128)S(1)} %fusion.44) | copy-start | bytes 86020
  145.5 10.4 %copy-start.8 = (f32[8,7,128]{2,1,0:T(8,128)}, f32[8,7,128]{2,1,0:T(8,128)S(1)}, u32[]{:S(2)}) copy-start(f32[8,7,128]{2,1,0:T(8,128)S(1)} %fusion.43) | copy-start | bytes 86020
  148.4 3.5 %collective-permute-start.14 = (f32[6,8,1,128]{3,1,2,0:T(8,128)S(1)}, f32[6,8,1,128]{3,1,2,0:T(8,128)S(1)}, u32[]{:S(2)}, u32[]{:S(2)}) collective-permute-start(f32[6,8,1,128]{3,1,2,0:T(8,128)S(1)} %bitcast.1398), channel_id=1, source_target_pairs={{12,0},{0,4},{4,8},{8,12},{13,1},{1,5},{5,9},{9,13},{14,2},{2,6},{... | collective-permute-start | bytes 73736 | tf_op jit(solution)/shard_map/ppermute | solution.py:58
  151.9 3.3 %collective-permute-start.15 = (f32[6,8,1,128]{3,1,2,0:T(8,128)S(1)}, f32[6,8,1,128]{3,1,2,0:T(8,128)S(1)}, u32[]{:S(2)}, u32[]{:S(2)}) collective-permute-start(f32[6,8,1,128]{3,1,2,0:T(8,128)S(1)} %bitcast.1394), channel_id=1, source_target_pairs={{4,0},{8,4},{12,8},{0,12},{5,1},{9,5},{13,9},{1,13},{6,2},{10,6},{... | collective-permute-start | bytes 73736 | tf_op jit(solution)/shard_map/ppermute | solution.py:58
  152.0 6.9 %copy-start.163 = (f32[1,8,1,128]{3,1,2,0:T(8,128)}, f32[1,8,1,128]{3,1,2,0:T(8,128)S(1)}, u32[]{:S(2)}) copy-start(f32[1,8,1,128]{3,1,2,0:T(8,128)S(1)} %get-tuple-element.734) | copy-start | bytes 12292
  162.8 7.3 %collective-permute-start.16 = (f32[6,8,8,1]{3,2,1,0:T(8,128)S(1)}, f32[6,8,8,1]{3,2,1,0:T(8,128)S(1)}, u32[]{:S(2)}, u32[]{:S(2)}) collective-permute-start(f32[6,8,8,1]{3,2,1,0:T(8,128)S(1)} %copy.1053), channel_id=1, source_target_pairs={{0,1},{1,2},{2,3},{4,5},{5,6},{6,7},{8,9},{9,10},{10,11},{12,13},{... | collective-permute-start | bytes 4616 | tf_op jit(solution)/shard_map/ppermute | solution.py:64
  168.0 8.7 %collective-permute-start.17 = (f32[6,8,8,1]{3,2,1,0:T(8,128)S(1)}, f32[6,8,8,1]{3,2,1,0:T(8,128)S(1)}, u32[]{:S(2)}, u32[]{:S(2)}) collective-permute-start(f32[6,8,8,1]{3,2,1,0:T(8,128)S(1)} %copy.1058), channel_id=1, source_target_pairs={{1,0},{2,1},{3,2},{5,4},{6,5},{7,6},{9,8},{10,9},{11,10},{13,12},{... | collective-permute-start | bytes 4616 | tf_op jit(solution)/shard_map/ppermute | solution.py:64
  170.2 6.6 %copy-start.103 = (f32[8,8,128]{2,1,0:T(8,128)S(1)}, f32[8,8,128]{2,1,0:T(8,128)}, u32[]{:S(2)}) copy-start(f32[8,8,128]{2,1,0:T(8,128)} %get-tuple-element.489) | copy-start | bytes 98308
  170.2 6.6 %copy-start.104 = (f32[8,8,128]{2,1,0:T(8,128)S(1)}, f32[8,8,128]{2,1,0:T(8,128)}, u32[]{:S(2)}) copy-start(f32[8,8,128]{2,1,0:T(8,128)} %get-tuple-element.490) | copy-start | bytes 98308
  171.0 5.8 %copy-start.58 = (f32[8,8,128]{2,1,0:T(8,128)S(1)}, f32[8,8,128]{2,1,0:T(8,128)}, u32[]{:S(2)}) copy-start(f32[8,8,128]{2,1,0:T(8,128)} %copy-done.57) | copy-start | bytes 98308
  171.0 5.8 %copy-start.87 = (f32[8,8,128]{2,1,0:T(8,128)S(1)}, f32[8,8,128]{2,1,0:T(8,128)}, u32[]{:S(2)}) copy-start(f32[8,8,128]{2,1,0:T(8,128)} %get-tuple-element.562) | copy-start | bytes 98308
  (196 other events, 266.2 us)
where the time goes:
time: 240 us; the launch traced here: 235 us
  local copies, waits for them, and re-layouts  93.5 us (39%)
  blocking collectives  40.1 us (17%)
  starting transfers between devices  40 us (17%)
  other arithmetic  31 us (13%)
  waiting for transfers between devices  23.9 us (10%)
  between operations  6.32 us (3%)
    unnamed x531, local copies, waits for them, and re-layouts  44.6 us
    psum x5, blocking collectives, one_axis_at_a_time(): return functools.reduce(lax.psum, axes, shard)  40.1 us
    ppermute x12, starting transfers between devices, shifted(): return lax.ppermute(block, axis, route)  27.1 us
    ppermute x6, waiting for transfers between devices, from_behind(): lax.ppermute(value, axis, [(source, source + steps) for source in range(l...  17.9 us
    ppermute x6, starting transfers between devices, from_behind(): lax.ppermute(value, axis, [(source, source + steps) for source in range(l...  12.9 us
    scatter x36, local copies, waits for them, and re-layouts, apply_walls(): single.at[:, :, plane].set(jnp.where(flag, back, single[:, :, plane]))  12 us
    unnamed x102, other arithmetic  8.25 us
    concatenate x16, other arithmetic, move_along(): jnp.concatenate([from_low[low_count], lax.slice_in_dim(single, 0, length...  7.25 us
  transfers between devices with their start and end apart: 18, of which 10 were waited for; matrix products, arithmetic and copies ran while one was open for 10% of the time, Pallas kernels for 0%

commit v1 on v0

v1 whole, which is shorter than its diff:
```python
import functools

import jax
import jax.numpy as jnp
import numpy as np
from jax import lax
from jax.experimental import pallas as pl
from jax.experimental.pallas import tpu as pltpu
from jax.sharding import PartitionSpec as P

MESH = pl.DeviceIdType.MESH
STEPS = 3
AXES = ("gx", "gy", "gz")

FLOW_SET = [
    (0, 0, 0),
    (1, 0, 0),
    (-1, 0, 0),
    (0, 1, 0),
    (0, -1, 0),
    (0, 0, 1),
    (0, 0, -1),
    (1, 1, 0),
    (-1, -1, 0),
    (1, -1, 0),
    (-1, 1, 0),
    (1, 0, 1),
    (-1, 0, -1),
    (1, 0, -1),
    (-1, 0, 1),
    (0, 1, 1),
    (0, -1, -1),
    (0, 1, -1),
    (0, -1, 1),
]
LATTICE = FLOW_SET + FLOW_SET[:7]
FLOWS = len(FLOW_SET)
POPS = len(LATTICE)
TAU_FLOW = 0.6
TAU_HEAT = 0.7
GRAVITY_LIFT = 0.01
HOT_WALL = 0.5
COLD_WALL = -0.5
DIFFUSIVITY = (TAU_HEAT - 0.5) / 4.0


def opposite(q):
    c = tuple(-v for v in LATTICE[q])
    return FLOW_SET.index(c) + (FLOWS if q >= FLOWS else 0)


def movers(axis, sign):
    return [q for q in range(POPS) if LATTICE[q][axis] == sign]


XP, XM = movers(0, 1), movers(0, -1)
YM = {1: movers(1, 1), -1: movers(1, -1)}
ZM = {1: movers(2, 1), -1: movers(2, -1)}
FACE = len(XP)
ORDER = XP + XM + [q for q in range(POPS) if LATTICE[q][0] == 0]
POS = {q: i for i, q in enumerate(ORDER)}
XY = [(q, LATTICE[q]) for q in range(FLOWS) if LATTICE[q][0] != 0 and LATTICE[q][1] != 0]
XY_SLOT = {q: i for i, (q, _) in enumerate(XY)}
ZOFF = [(0, 0), (1, 0), (-1, 0), (0, 1), (0, -1)]
LANE0 = 8


def messages():
    out = [("x", 1, (1, 0, 0)), ("x", -1, (-1, 0, 0)), ("y", 1, (0, 1, 0)), ("y", -1, (0, -1, 0))]
    out += [("xy", q, c) for q, c in XY]
    out += [("z", (cz, i), (dx, dy, cz)) for cz in (1, -1) for i, (dx, dy) in enumerate(ZOFF)]
    return out


MESSAGES = messages()


def collide(f):
    s, d = {}, {}
    for q in range(1, FLOWS, 2):
        s[q] = f[q] + f[q + 1]
        d[q] = f[q] - f[q + 1]
    rho = (((s[1] + s[3]) + (s[5] + s[7])) + ((s[9] + s[11]) + (s[13] + s[15]))) + (s[17] + f[0])
    jx = (d[1] + d[7]) + (d[9] + d[11]) + d[13]
    jy = (d[3] + d[7]) + (d[15] + d[17]) - d[9]
    jz = (d[5] + d[11]) + (d[15] - d[13]) - d[17]
    g = [f[FLOWS + i] for i in range(7)]
    warmth = ((g[0] + g[1]) + (g[2] + g[3])) + ((g[4] + g[5]) + g[6])
    force = GRAVITY_LIFT * rho * warmth
    inv = 1.0 / rho
    ux = jx * inv
    uy = jy * inv
    uz = (jz + 0.5 * force) * inv

    w2 = 1.0 / 36.0
    keep = 1.0 - 1.0 / TAU_FLOW
    r = (w2 / TAU_FLOW) * rho
    sf = (w2 * (1.0 - 0.5 / TAU_FLOW)) * force
    r3 = 3.0 * r
    rx, ry, rz = r3 * ux, r3 * uy, r3 * uz
    sf3 = 3.0 * sf
    ax, ay, az = rx, ry, rz + sf3
    bx, by, bz = 1.5 * rx, 1.5 * ry, 1.5 * rz + 3.0 * sf3
    qx, qy, qz = ux * bx, uy * by, uz * bz
    usq = rx * ux + ry * uy + rz * uz
    base = r - 0.5 * usq - sf3 * uz
    cxy = ux * by + uy * bx
    cxz = ux * bz + uz * bx
    cyz = uy * bz + uz * by

    out = {0: keep * f[0] + 12.0 * base}

    def pair(q, even, odd):
        out[q] = keep * f[q] + (even + odd)
        out[q + 1] = keep * f[q + 1] + (even - odd)

    pair(1, 2.0 * (base + qx), 2.0 * ax)
    pair(3, 2.0 * (base + qy), 2.0 * ay)
    pair(5, 2.0 * (base + qz), 2.0 * az)
    exy = base + (qx + qy)
    exz = base + (qx + qz)
    eyz = base + (qy + qz)
    pair(7, exy + cxy, ax + ay)
    pair(9, exy - cxy, ax - ay)
    pair(11, exz + cxz, ax + az)
    pair(13, exz - cxz, ax - az)
    pair(15, eyz + cyz, ay + az)
    pair(17, eyz - cyz, ay - az)

    keep_heat = 1.0 - 1.0 / TAU_HEAT
    t8 = (0.125 / TAU_HEAT) * warmth
    t2 = 4.0 * t8
    out[FLOWS] = keep_heat * g[0] + 2.0 * t8
    for i, u in ((1, ux), (3, uy), (5, uz)):
        odd = t2 * u
        out[FLOWS + i] = keep_heat * g[i] + (t8 + odd)
        out[FLOWS + i + 1] = keep_heat * g[i + 1] + (t8 - odd)
    return out


def flux(f):
    total = lambda values: functools.reduce(lambda a, b: a + b, values)
    rho = total([f[q] for q in range(FLOWS)])
    jz = total([f[q] for q in range(FLOWS) if LATTICE[q][2] == 1]) - total(
        [f[q] for q in range(FLOWS) if LATTICE[q][2] == -1]
    )
    warmth = total([f[q] for q in range(FLOWS, POPS)])
    force = GRAVITY_LIFT * rho * warmth
    return (jz + 0.5 * force) / rho * warmth


def kernel(
    shape,
    sizes,
    flow_in,
    heat_in,
    flow_out,
    heat_out,
    nusselt,
    held,
    post,
    ysend,
    yrecv,
    ydiag,
    zsend,
    zrecv,
    yedge,
    red_a,
    red_b,
    in_sem,
    out_sem,
    send_sem,
    recv_sem,
    send_a,
    recv_a,
    send_b,
    recv_b,
):
    nx, ny, nz = shape
    planes, rows, lanes = sizes
    me = tuple(lax.axis_index(a) for a in AXES)

    def at(off):
        return tuple(
            m if d == 0 else lax.rem(m + (d % n), n) for m, d, n in zip(me, off, shape)
        )

    loads = [
        pltpu.make_async_copy(flow_in, held.at[pl.ds(0, FLOWS)], in_sem.at[0]),
        pltpu.make_async_copy(heat_in, held.at[pl.ds(FLOWS, 7)], in_sem.at[1]),
    ]
    for c in loads:
        c.start()

    offsets = {tuple(d % n for d, n in zip(off, shape)) for _, _, off in MESSAGES}
    offsets |= {(0, dy, dz) for dy in range(ny) for dz in range(nz)}
    offsets |= {(dx, 0, 0) for dx in range(nx)}
    offsets -= {(0, 0, 0)}
    barrier = pltpu.get_barrier_semaphore()
    for off in sorted(offsets):
        pl.semaphore_signal(barrier, inc=1, device_id=at(off), device_id_type=MESH)

    lane = lax.broadcasted_iota(jnp.int32, (rows, lanes), 1)
    row = lax.broadcasted_iota(jnp.int32, (rows, lanes), 0)
    is_bottom = me[2] == 0
    is_top = me[2] == nz - 1
    end_lane = {1: lane == 0, -1: lane == lanes - 1}
    wall = {1: jnp.logical_and(end_lane[1], is_bottom), -1: jnp.logical_and(end_lane[-1], is_top)}
    end_row = {1: row == 0, -1: row == rows - 1}
    far_row = {1: row == rows - 1, -1: row == 0}

    def turn(v, c, axis):
        n = rows if axis == 0 else lanes
        return pltpu.roll(v, 1 if c == 1 else n - 1, axis)

    def plane(x):
        return pl.ds(pl.multiple_of((x + 1) * rows, rows), rows)

    def keep(s, x, out, packed):
        for q in range(POPS):
            post[s, POS[q], plane(x), :] = out[q]
        result = []
        for cz, tile in zip((1, -1), packed):
            for j, q in enumerate(ZM[cz]):
                k = LANE0 + j * planes + x
                tile = jnp.where(lane == k, pltpu.roll(out[q], k + (1 if cz == 1 else 0), 1), tile)
            result.append(tile)
        return tuple(result)

    def copy(s, m):
        kind, slot, off = MESSAGES[m]
        if kind == "x":
            group = pl.ds(0 if slot == 1 else FACE, FACE)
            src, dst = (planes, 0) if slot == 1 else (1, planes + 1)
            src = post.at[s, group, pl.ds(src * rows, rows)]
            dst = post.at[s, group, pl.ds(dst * rows, rows)]
        elif kind == "y":
            src, dst = (b.at[s, 0 if slot == 1 else 1] for b in (ysend, yrecv))
        elif kind == "xy":
            cy = off[1]
            src = ysend.at[s, 0 if cy == 1 else 1, YM[cy].index(slot)]
            dst = ydiag.at[s, XY_SLOT[slot]]
        else:
            cz, i = slot
            src = zsend.at[s, 0 if cz == 1 else 1]
            dst = zrecv.at[s, 0 if cz == 1 else 1, i]
        return pltpu.make_async_remote_copy(
            src_ref=src,
            dst_ref=dst,
            send_sem=send_sem.at[s, m],
            recv_sem=recv_sem.at[s, m],
            device_id=at(off),
            device_id_type=MESH,
        )

    def of_kind(dz):
        return [m for m, (_, _, off) in enumerate(MESSAGES) if off[2] == dz]

    def send(s, packed):
        for i, cy in enumerate((1, -1)):
            first = rows + (rows - 1 if cy == 1 else 0)
            for j, q in enumerate(YM[cy]):
                ysend[s, i, j] = post[s, POS[q], pl.ds(first, planes, stride=rows), :]
        zsend[s, 0] = packed[0]
        zsend[s, 1] = packed[1]

    def start(s):
        for m in of_kind(0):
            copy(s, m).start()

        @pl.when(jnp.logical_not(is_top))
        def _():
            for m in of_kind(1):
                copy(s, m).start()

        @pl.when(jnp.logical_not(is_bottom))
        def _():
            for m in of_kind(-1):
                copy(s, m).start()

    def receive(s):
        for m in of_kind(0):
            copy(s, m).wait_recv()

        @pl.when(jnp.logical_not(is_bottom))
        def _():
            for m in of_kind(1):
                copy(s, m).wait_recv()

        @pl.when(jnp.logical_not(is_top))
        def _():
            for m in of_kind(-1):
                copy(s, m).wait_recv()

    def drain(s):
        for m in of_kind(0):
            copy(s, m).wait_send()

        @pl.when(jnp.logical_not(is_top))
        def _():
            for m in of_kind(1):
                copy(s, m).wait_send()

        @pl.when(jnp.logical_not(is_bottom))
        def _():
            for m in of_kind(-1):
                copy(s, m).wait_send()

    def edges(s):
        for i, cy in enumerate((1, -1)):
            for j, q in enumerate(YM[cy]):
                cx = LATTICE[q][0]
                tile = yrecv[s, i, j]
                if cx:
                    tile = turn(jnp.where(far_row[cx], ydiag[s, XY_SLOT[q]], tile), cx, 0)
                yedge[s, i, j] = tile
        tiles = {}
        for i, cz in enumerate((1, -1)):
            own = zrecv[s, i, 0]
            tile = own
            for j, q in enumerate(ZM[cz]):
                cx, cy, _ = LATTICE[q]
                if cx == 0 and cy == 0:
                    continue
                low = LANE0 + j * planes
                other = zrecv[s, i, ZOFF.index((cx, cy))]
                if cx:
                    near = low + (0 if cx == 1 else planes - 1)
                    back = (lanes - planes + 1) if cx == 1 else planes - 1
                    moved = jnp.where(lane == near, pltpu.roll(other, back, 1), turn(own, cx, 1))
                else:
                    moved = turn(jnp.where(far_row[cy], other, own), cy, 0)
                tile = jnp.where(jnp.logical_and(lane >= low, lane < low + planes), moved, tile)
            tiles[cz] = tile
        return tiles

    def stream(s, x, tiles):
        f = {}
        for q in range(POPS):
            cx, cy, cz = LATTICE[q]
            v = post[s, POS[q], plane(x - cx), :]
            if cy:
                i, j = (0 if cy == 1 else 1), YM[cy].index(q)
                edge = jnp.broadcast_to(yedge[s, i, j, pl.ds(x, 1), :], (rows, lanes))
                v = jnp.where(end_row[cy], edge, turn(v, cy, 0))
            if cz:
                k = LANE0 + ZM[cz].index(q) * planes + x
                edge = pltpu.roll(tiles[cz], (lanes if cz == 1 else lanes - 1) - k, 1)
                back = post[s, POS[opposite(q)], plane(x), :]
                if q >= FLOWS:
                    back = 0.25 * (HOT_WALL if cz == 1 else COLD_WALL) - back
                v = jnp.where(wall[cz], back, jnp.where(end_lane[cz], edge, turn(v, cz, 1)))
            f[q] = v
        return f

    blank = jnp.zeros((rows, lanes), jnp.float32)

    for c in loads:
        c.wait()

    def first(x, packed):
        at_x = pl.ds(pl.multiple_of(x * rows, rows), rows)
        return keep(0, x, collide({q: held[q, at_x, :] for q in range(POPS)}), packed)

    send(0, lax.fori_loop(0, planes, first, (blank, blank)))
    pl.semaphore_wait(barrier, len(offsets))
    start(0)

    for s in range(1, STEPS):
        receive(s - 1)
        tiles = edges(s - 1)

        def middle(x, packed, s=s, tiles=tiles):
            return keep(s, x, collide(stream(s - 1, x, tiles)), packed)

        send(s, lax.fori_loop(0, planes, middle, (blank, blank)))
        start(s)

    receive(STEPS - 1)
    tiles = edges(STEPS - 1)

    def last(x, acc):
        f = stream(STEPS - 1, x, tiles)
        at_x = pl.ds(pl.multiple_of(x * rows, rows), rows)
        for q in range(POPS):
            held[q, at_x, :] = f[q]
        return acc + flux(f)

    acc = lax.fori_loop(0, planes, last, blank)
    stores = [
        pltpu.make_async_copy(held.at[pl.ds(0, FLOWS)], flow_out, out_sem.at[0]),
        pltpu.make_async_copy(held.at[pl.ds(FLOWS, 7)], heat_out, out_sem.at[1]),
    ]
    for c in stores:
        c.start()

    def exchange(value, buf, index, peers, sends, recvs):
        buf[index] = value
        count = buf.shape[0]

        def to(d):
            return pltpu.make_async_remote_copy(
                src_ref=buf.at[index],
                dst_ref=buf.at[index],
                send_sem=sends.at[d],
                recv_sem=recvs.at[d],
                device_id=peers[d],
                device_id_type=MESH,
            )

        for d in range(1, count):
            to(d).start()
        for d in range(1, count):
            to(d).wait_recv()
        total = buf[0]
        for d in range(1, count):
            total = total + buf[d]
        for d in range(1, count):
            to(d).wait_send()
        return total

    part = jnp.sum(acc, axis=0, keepdims=True)
    peers = [at((0, d // nz, d % nz)) for d in range(ny * nz)]
    part = exchange(part, red_a, me[1] * nz + me[2], peers, send_a, recv_a)
    peers = [at((d, 0, 0)) for d in range(nx)]
    part = exchange(part, red_b, me[0], peers, send_b, recv_b)
    total = jnp.sum(part)
    cells = nx * planes * ny * rows * nz * lanes
    height = nz * lanes
    nusselt[0, 0] = 1.0 + (height / (DIFFUSIVITY * (HOT_WALL - COLD_WALL)) / cells) * total

    for s in range(STEPS):
        drain(s)
    for c in stores:
        c.wait()


def per_device(shape, flow_pops, heat_pops):
    nx, ny, nz = shape
    _, planes, rows, lanes = flow_pops.shape
    flat = (planes * rows, lanes)
    dma = pltpu.SemaphoreType.DMA
    tile = (rows, lanes)
    vmem = lambda *dims: pltpu.VMEM(dims, jnp.float32)
    flow, heat, nusselt = pl.pallas_call(
        functools.partial(kernel, shape, (planes, rows, lanes)),
        out_shape=(
            jax.ShapeDtypeStruct((FLOWS,) + flat, jnp.float32),
            jax.ShapeDtypeStruct((7,) + flat, jnp.float32),
            jax.ShapeDtypeStruct((1, 1), jnp.float32),
        ),
        in_specs=[pl.BlockSpec(memory_space=pl.ANY)] * 2,
        out_specs=(
            pl.BlockSpec(memory_space=pl.ANY),
            pl.BlockSpec(memory_space=pl.ANY),
            pl.BlockSpec(memory_space=pltpu.SMEM),
        ),
        scratch_shapes=[
            vmem(POPS, *flat),
            vmem(STEPS, POPS, (planes + 2) * rows, lanes),
            vmem(STEPS, 2, FACE, *tile),
            vmem(STEPS, 2, FACE, *tile),
            vmem(STEPS, len(XY), *tile),
            vmem(STEPS, 2, *tile),
            vmem(STEPS, 2, len(ZOFF), *tile),
            vmem(STEPS, 2, FACE, *tile),
            vmem(ny * nz, 1, lanes),
            vmem(nx, 1, lanes),
            dma((2,)),
            dma((2,)),
            dma((STEPS, len(MESSAGES))),
            dma((STEPS, len(MESSAGES))),
            dma((ny * nz,)),
            dma((ny * nz,)),
            dma((nx,)),
            dma((nx,)),
        ],
        compiler_params=pltpu.CompilerParams(collective_id=0, has_side_effects=True),
        name="lattice_steps",
    )(flow_pops.reshape((FLOWS,) + flat), heat_pops.reshape((7,) + flat))
    return flow.reshape(flow_pops.shape), heat.reshape(heat_pops.shape), nusselt.reshape(())


def solution(mesh):
    shape = tuple(mesh.shape[a] for a in AXES)
    spec = P(None, *AXES)
    return jax.shard_map(
        functools.partial(per_device, shape),
        mesh=mesh,
        in_specs=(spec, spec),
        out_specs=(spec, spec, P()),
        check_vma=False,
    )
```

time: 240 us -> 47.4 us (0.20); the launches traced: 235 us -> 47.2 us
  local copies, waits for them, and re-layouts: 93.5 us -> 2.69 us
  Pallas kernels: 0 us -> 42.2 us
  blocking collectives: 40.1 us -> 0 us
  starting transfers between devices: 40 us -> 0 us
  other arithmetic: 31 us -> 0 us
  waiting for transfers between devices: 23.9 us -> 0 us
  between operations: 6.32 us -> 2.33 us
    pallas_call x0 -> x1, Pallas kernels: none -> 42.2 us  [per_device(): pl.pallas_call(functools.partial(kernel, shape, (planes, rows, lanes)), o...]
    unnamed x531 -> x4, local copies, waits for them, and re-layouts: 44.6 us -> 2.69 us
    psum x5 -> x0, blocking collectives: 40.1 us -> none  [one_axis_at_a_time(): return functools.reduce(lax.psum, axes, shard)]
    ppermute x18 -> x0, starting transfers between devices: 40 us -> none  [the longest x12 27.1 us: shifted(): return lax.ppermute(block, axis, route)]
    ppermute x18 -> x0, waiting for transfers between devices: 23.9 us -> none  [the longest x6 17.9 us: from_behind(): lax.ppermute(value, axis, [(source, source + steps) for source in range(l...]
    slice x44 -> x0, local copies, waits for them, and re-layouts: 17.3 us -> none  [the longest x9 5.14 us: first_plane(): return lax.slice_in_dim(pops, 0, 1, axis=axis_col + 1)[falling(axis_col)]]
    gather x24 -> x0, local copies, waits for them, and re-layouts: 13.9 us -> none  [the longest x12 6.94 us: last_plane(): lax.slice_in_dim(pops, length - 1, length, axis=axis_col + 1)]
    concatenate x33 -> x0, other arithmetic: 12.6 us -> none  [the longest x16 7.25 us: move_along(): jnp.concatenate([from_low[low_count], lax.slice_in_dim(single, 0, length...]
  transfers between devices with their start and end apart: 18 -> 0, of which waited for: 10 -> 0; matrix products, arithmetic and copies ran while one was open for 10% -> 0% of each run, Pallas kernels for 0% -> 0%
where the time goes in v1:
time: 47.4 us; the launch traced here: 47.2 us
  Pallas kernels  42.2 us (89%)
  local copies, waits for them, and re-layouts  2.69 us (6%)
  between operations  2.33 us (5%)
    pallas_call x1, Pallas kernels, per_device(): pl.pallas_call(functools.partial(kernel, shape, (planes, rows, lanes)), o...  42.2 us
    unnamed x4, local copies, waits for them, and re-layouts  2.69 us

profile of v1, /device:TPU:1, one launch (start us, length us, event | category | flops | bytes accessed | tf_op | source)
XLA Modules:
  0.0 47.2 jit_solution(3750403434546886871)
XLA Ops:
  0.6 42.2 %lattice_steps.1 = (f32[19,64,128]{2,1,0:T(8,128)}, f32[7,64,128]{2,1,0:T(8,128)}, f32[1,1]{1,0:T(1,128)}) custom-call(f32[19,64,128]{2,1,0:T(8,128)} %bitcast.6, f32[7,64,128]{2,1,0:T(8,128)} %bitcast.8), custom_call_target="tpu_custom_call" | custom-call | tf_op jit(solution)/shard_map/lattice_steps/pallas_call | solution.py:445
  42.9 0.0 copy-start
  42.9 2.0 %copy.8 = f32[19,8,8,128]{3,2,1,0:T(8,128)} copy(f32[19,8,8,128]{3,2,1,0:T(8,128)} %bitcast.5) | data formatting | bytes 1245184
  44.9 0.0 copy-done
  44.9 0.7 %copy.9 = f32[7,8,8,128]{3,2,1,0:T(8,128)} copy(f32[7,8,8,128]{3,2,1,0:T(8,128)S(1)} %bitcast.7) | data formatting | bytes 458752
Async XLA Ops:
  42.9 2.0 %copy-start = (f32[7,64,128]{2,1,0:T(8,128)S(1)}, f32[7,64,128]{2,1,0:T(8,128)}, u32[]{:S(2)}) copy-start(f32[7,64,128]{2,1,0:T(8,128)} %get-tuple-element.7) | copy-start | bytes 688132

commit v2 on v1

v2 whole, which is shorter than its diff:
```python
import functools

import jax
import jax.numpy as jnp
import numpy as np
from jax import lax
from jax.experimental import pallas as pl
from jax.experimental.pallas import tpu as pltpu
from jax.sharding import PartitionSpec as P

MESH = pl.DeviceIdType.MESH
STEPS = 3
AXES = ("gx", "gy", "gz")

FLOW_SET = [
    (0, 0, 0),
    (1, 0, 0),
    (-1, 0, 0),
    (0, 1, 0),
    (0, -1, 0),
    (0, 0, 1),
    (0, 0, -1),
    (1, 1, 0),
    (-1, -1, 0),
    (1, -1, 0),
    (-1, 1, 0),
    (1, 0, 1),
    (-1, 0, -1),
    (1, 0, -1),
    (-1, 0, 1),
    (0, 1, 1),
    (0, -1, -1),
    (0, 1, -1),
    (0, -1, 1),
]
LATTICE = FLOW_SET + FLOW_SET[:7]
FLOWS = len(FLOW_SET)
POPS = len(LATTICE)
TAU_FLOW = 0.6
TAU_HEAT = 0.7
GRAVITY_LIFT = 0.01
HOT_WALL = 0.5
COLD_WALL = -0.5
DIFFUSIVITY = (TAU_HEAT - 0.5) / 4.0


def opposite(q):
    c = tuple(-v for v in LATTICE[q])
    return FLOW_SET.index(c) + (FLOWS if q >= FLOWS else 0)


def movers(axis, sign):
    return [q for q in range(POPS) if LATTICE[q][axis] == sign]


XP, XM = movers(0, 1), movers(0, -1)
YM = {1: movers(1, 1), -1: movers(1, -1)}
ZM = {1: movers(2, 1), -1: movers(2, -1)}
FACE = len(XP)
ORDER = XP + XM + [q for q in range(POPS) if LATTICE[q][0] == 0]
POS = {q: i for i, q in enumerate(ORDER)}
XY = [q for q in range(FLOWS) if LATTICE[q][0] != 0 and LATTICE[q][1] != 0]
XZ = [q for q in range(FLOWS) if LATTICE[q][0] != 0 and LATTICE[q][2] != 0]
LANE0 = 8


def messages():
    out = [("x", 1, (1, 0, 0)), ("x", -1, (-1, 0, 0))]
    out += [("xz", q, LATTICE[q]) for q in XZ]
    out += [("xy", q, LATTICE[q]) for q in XY]
    out += [("z", (cz, cy), (0, cy, cz)) for cz in (1, -1) for cy in (1, -1, 0)]
    out += [("y", 1, (0, 1, 0)), ("y", -1, (0, -1, 0))]
    return out


MESSAGES = messages()
END_PLANES = ("x", "xy", "xz")
ALL_PLANES = ("y", "z")


def collide(f):
    s, d = {}, {}
    for q in range(1, FLOWS, 2):
        s[q] = f[q] + f[q + 1]
        d[q] = f[q] - f[q + 1]
    rho = (((s[1] + s[3]) + (s[5] + s[7])) + ((s[9] + s[11]) + (s[13] + s[15]))) + (s[17] + f[0])
    jx = (d[1] + d[7]) + (d[9] + d[11]) + d[13]
    jy = (d[3] + d[7]) + (d[15] + d[17]) - d[9]
    jz = (d[5] + d[11]) + (d[15] - d[13]) - d[17]
    g = [f[FLOWS + i] for i in range(7)]
    warmth = ((g[0] + g[1]) + (g[2] + g[3])) + ((g[4] + g[5]) + g[6])
    force = GRAVITY_LIFT * rho * warmth
    inv = 1.0 / rho
    ux = jx * inv
    uy = jy * inv
    uz = (jz + 0.5 * force) * inv

    w2 = 1.0 / 36.0
    keep = 1.0 - 1.0 / TAU_FLOW
    r = (w2 / TAU_FLOW) * rho
    sf = (w2 * (1.0 - 0.5 / TAU_FLOW)) * force
    r3 = 3.0 * r
    rx, ry, rz = r3 * ux, r3 * uy, r3 * uz
    sf3 = 3.0 * sf
    ax, ay, az = rx, ry, rz + sf3
    bx, by, bz = 1.5 * rx, 1.5 * ry, 1.5 * rz + 3.0 * sf3
    qx, qy, qz = ux * bx, uy * by, uz * bz
    usq = rx * ux + ry * uy + rz * uz
    base = r - 0.5 * usq - sf3 * uz
    cxy = ux * by + uy * bx
    cxz = ux * bz + uz * bx
    cyz = uy * bz + uz * by

    out = {0: keep * f[0] + 12.0 * base}

    def pair(q, even, odd):
        out[q] = keep * f[q] + (even + odd)
        out[q + 1] = keep * f[q + 1] + (even - odd)

    pair(1, 2.0 * (base + qx), 2.0 * ax)
    pair(3, 2.0 * (base + qy), 2.0 * ay)
    pair(5, 2.0 * (base + qz), 2.0 * az)
    exy = base + (qx + qy)
    exz = base + (qx + qz)
    eyz = base + (qy + qz)
    pair(7, exy + cxy, ax + ay)
    pair(9, exy - cxy, ax - ay)
    pair(11, exz + cxz, ax + az)
    pair(13, exz - cxz, ax - az)
    pair(15, eyz + cyz, ay + az)
    pair(17, eyz - cyz, ay - az)

    keep_heat = 1.0 - 1.0 / TAU_HEAT
    t8 = (0.125 / TAU_HEAT) * warmth
    t2 = 4.0 * t8
    out[FLOWS] = keep_heat * g[0] + 2.0 * t8
    for i, u in ((1, ux), (3, uy), (5, uz)):
        odd = t2 * u
        out[FLOWS + i] = keep_heat * g[i] + (t8 + odd)
        out[FLOWS + i + 1] = keep_heat * g[i + 1] + (t8 - odd)
    return out


def flux(f):
    total = lambda values: functools.reduce(lambda a, b: a + b, values)
    rho = total([f[q] for q in range(FLOWS)])
    jz = total([f[q] for q in range(FLOWS) if LATTICE[q][2] == 1]) - total(
        [f[q] for q in range(FLOWS) if LATTICE[q][2] == -1]
    )
    warmth = total([f[q] for q in range(FLOWS, POPS)])
    force = GRAVITY_LIFT * rho * warmth
    return (jz + 0.5 * force) / rho * warmth


def kernel(
    shape,
    sizes,
    flow_in,
    heat_in,
    flow_out,
    heat_out,
    nusselt,
    held,
    post,
    ysend,
    yrecv,
    ydiag,
    zsend,
    zrecv,
    zdiag,
    part,
    parts,
    total,
    in_sem,
    send_sem,
    recv_sem,
    part_send,
    part_recv,
    total_send,
    total_recv,
):
    nx, ny, nz = shape
    planes, rows, lanes = sizes
    me = tuple(lax.axis_index(a) for a in AXES)
    count = nx * ny * nz
    group = ny * nz
    roots = (nx // 4) * group
    my_index = me[0] * group + me[1] * nz + me[2]
    is_root = me[0] < nx // 4

    def at(off):
        return tuple(m if d == 0 else lax.rem(m + (d % n), n) for m, d, n in zip(me, off, shape))

    offsets = [off for off in np.ndindex(3, 3, 3) if off != (1, 1, 1)]
    offsets = [tuple(d - 1 for d in off) for off in offsets if 1 in off]
    barrier = pltpu.get_barrier_semaphore()
    for off in offsets:
        pl.semaphore_signal(barrier, inc=1, device_id=at(off), device_id_type=MESH)

    inner, ends = range(1, planes - 1), (0, planes - 1)
    blocks = [(0, 1), (planes - 1, 1), (1, planes - 2)]
    loads = []
    for i, (x, n) in enumerate(blocks):
        some = pl.ds(x * rows, n * rows)
        for j, (ref, low, n) in enumerate(((flow_in, 0, FLOWS), (heat_in, FLOWS, 7))):
            loads.append(
                pltpu.make_async_copy(ref.at[:, some], held.at[pl.ds(low, n), some], in_sem.at[2 * i + j])
            )
    for c in loads:
        c.start()

    @pl.when(is_root)
    def _():
        def tell(d, carry):
            pl.semaphore_signal(
                barrier,
                inc=1,
                device_id=lax.rem(my_index + d, count),
                device_id_type=pl.DeviceIdType.LOGICAL,
            )
            return carry

        lax.fori_loop(1, count, tell, 0)

    lane = lax.broadcasted_iota(jnp.int32, (rows, lanes), 1)
    row = lax.broadcasted_iota(jnp.int32, (rows, lanes), 0)
    is_bottom = me[2] == 0
    is_top = me[2] == nz - 1
    end_lane = {1: lane == 0, -1: lane == lanes - 1}
    wall = {1: jnp.logical_and(end_lane[1], is_bottom), -1: jnp.logical_and(end_lane[-1], is_top)}
    end_row = {1: row == 0, -1: row == rows - 1}
    far_row = {1: rows - 1, -1: 0}
    side = {1: 0, -1: 1}

    def turn(v, c, axis):
        n = rows if axis == 0 else lanes
        return pltpu.roll(v, 1 if c == 1 else n - 1, axis)

    def plane(x):
        return pl.ds((x + 1) * rows, rows)

    def keep(s, x, out, packed):
        for q in range(POPS):
            post[s, POS[q], plane(x), :] = out[q]
        for cz in (1, -1):
            for j, q in enumerate(ZM[cz]):
                k = LANE0 + j * planes + x
                packed[cz] = jnp.where(lane == k, pltpu.roll(out[q], k + (1 if cz == 1 else 0), 1), packed[cz])

    def copy(s, m):
        kind, slot, off = MESSAGES[m]
        if kind == "x":
            some = pl.ds(0 if slot == 1 else FACE, FACE)
            src, dst = (planes - 1, -1) if slot == 1 else (0, planes)
            src, dst = post.at[s, some, plane(src)], post.at[s, some, plane(dst)]
        elif kind == "y":
            src, dst = ysend.at[s, side[slot]], yrecv.at[s, side[slot]]
        elif kind == "z":
            cz, cy = slot
            src, dst = zsend.at[s, side[cz]], zrecv.at[s, side[cz], cy + 1]
        else:
            src = post.at[s, POS[slot], plane(planes - 1 if off[0] == 1 else 0)]
            dst = ydiag.at[s, XY.index(slot)] if kind == "xy" else zdiag.at[s, XZ.index(slot)]
        return pltpu.make_async_remote_copy(
            src_ref=src,
            dst_ref=dst,
            send_sem=send_sem.at[s, m],
            recv_sem=recv_sem.at[s, m],
            device_id=at(off),
            device_id_type=MESH,
        )

    def of_kind(kinds, dz):
        return [m for m, (kind, _, off) in enumerate(MESSAGES) if kind in kinds and off[2] == dz]

    def each(s, kinds, act, up, down):
        for dz, when in ((1, up), (-1, down)):
            if of_kind(kinds, dz):

                @pl.when(when)
                def _():
                    for m in of_kind(kinds, dz):
                        act(copy(s, m))

        for m in of_kind(kinds, 0):
            act(copy(s, m))

    def start(s, kinds):
        each(s, kinds, lambda c: c.start(), jnp.logical_not(is_top), jnp.logical_not(is_bottom))

    def receive(s, kinds):
        each(s, kinds, lambda c: c.wait_recv(), jnp.logical_not(is_bottom), jnp.logical_not(is_top))

    def drain(s, kinds):
        each(s, kinds, lambda c: c.wait_send(), jnp.logical_not(is_top), jnp.logical_not(is_bottom))

    def pack(s, packed):
        for cy in (1, -1):
            first = rows + far_row[cy]
            for j, q in enumerate(YM[cy]):
                ysend[s, side[cy], j] = post[s, POS[q], pl.ds(first, planes, stride=rows), :]
        for cz in (1, -1):
            zsend[s, side[cz]] = packed[cz]

    def z_faces(s):
        tiles = {}
        for cz in (1, -1):
            own = zrecv[s, side[cz], 1]
            tiles[cz, 0] = own
            for cy in (1, -1):
                other = zrecv[s, side[cz], cy + 1]
                tiles[cz, cy] = turn(jnp.where(row == far_row[cy], other, own), cy, 0)
        return tiles

    def stream(s, x, tiles):
        f = {}
        for q in range(POPS):
            cx, cy, cz = LATTICE[q]
            v = post[s, POS[q], plane(x - cx), :]
            inside = 0 <= x - cx < planes
            if cy:
                if inside:
                    edge = yrecv[s, side[cy], YM[cy].index(q), pl.ds(x - cx, 1), :]
                else:
                    edge = ydiag[s, XY.index(q), pl.ds(far_row[cy], 1), :]
                v = jnp.where(end_row[cy], jnp.broadcast_to(edge, (rows, lanes)), turn(v, cy, 0))
            if cz:
                if inside:
                    k = LANE0 + ZM[cz].index(q) * planes + x - cx
                    edge = pltpu.roll(tiles[cz, cy], (lanes if cz == 1 else lanes - 1) - k, 1)
                else:
                    edge = turn(zdiag[s, XZ.index(q)], cz, 1)
                back = post[s, POS[opposite(q)], plane(x), :]
                if q >= FLOWS:
                    back = 0.25 * (HOT_WALL if cz == 1 else COLD_WALL) - back
                v = jnp.where(wall[cz], back, jnp.where(end_lane[cz], edge, turn(v, cz, 1)))
            f[q] = v
        return f

    blank = jnp.zeros((rows, lanes), jnp.float32)

    def first(x, packed):
        keep(0, x, collide({q: held[q, pl.ds(x * rows, rows), :] for q in range(POPS)}), packed)

    packed = {1: blank, -1: blank}
    for c in loads[:4]:
        c.wait()
    for x in ends:
        first(x, packed)
    pl.semaphore_wait(barrier, len(offsets) + roots - is_root.astype(jnp.int32))
    start(0, END_PLANES)
    for c in loads[4:]:
        c.wait()
    for x in inner:
        first(x, packed)
    pack(0, packed)
    start(0, ALL_PLANES)

    for s in range(1, STEPS):
        packed = {1: blank, -1: blank}
        receive(s - 1, ALL_PLANES)
        tiles = z_faces(s - 1)
        for x in inner:
            keep(s, x, collide(stream(s - 1, x, tiles)), packed)
        receive(s - 1, END_PLANES)
        for x in ends:
            keep(s, x, collide(stream(s - 1, x, tiles)), packed)
        start(s, END_PLANES)
        pack(s, packed)
        start(s, ALL_PLANES)

    def last(x, tiles):
        f = stream(STEPS - 1, x, tiles)
        for q in range(FLOWS):
            flow_out[q, pl.ds(x * rows, rows), :] = f[q]
        for q in range(FLOWS, POPS):
            heat_out[q - FLOWS, pl.ds(x * rows, rows), :] = f[q]
        return flux(f)

    receive(STEPS - 1, ALL_PLANES)
    tiles = z_faces(STEPS - 1)
    acc = blank
    for x in inner:
        acc = acc + last(x, tiles)
    receive(STEPS - 1, END_PLANES)
    for x in ends:
        acc = acc + last(x, tiles)

    mine = jnp.sum(acc, axis=0, keepdims=True)
    part[0] = mine
    parts[my_index] = mine
    base = lax.rem(my_index, roots)

    def to_root(d, k):
        return pltpu.make_async_remote_copy(
            src_ref=part.at[0],
            dst_ref=parts.at[my_index],
            send_sem=part_send.at[k],
            recv_sem=part_recv.at[0],
            device_id=lax.rem(base + d, roots),
            device_id_type=pl.DeviceIdType.LOGICAL,
        )

    for d in range(1, roots):
        to_root(d, 0).start()

    @pl.when(jnp.logical_not(is_root))
    def _():
        to_root(0, 1).start()

    half = nx // 2
    served = [me[0] + half, half - 1 - me[0], nx - 1 - me[0]]

    def to_served(i):
        return pltpu.make_async_remote_copy(
            src_ref=total.at[0],
            dst_ref=total.at[0],
            send_sem=total_send.at[i],
            recv_sem=total_recv.at[0],
            device_id=(served[i], me[1], me[2]),
            device_id_type=MESH,
        )

    def whole(n, k):
        some = parts.at[pl.ds(0, n)]
        return pltpu.make_async_remote_copy(
            src_ref=some,
            dst_ref=some,
            send_sem=part_send.at[k],
            recv_sem=part_recv.at[0],
            device_id=0,
            device_id_type=pl.DeviceIdType.LOGICAL,
        )

    @pl.when(is_root)
    def _():
        whole(count - 1, 0).wait_recv()
        sums = [parts[i] for i in range(8)]
        for i in range(8, count):
            sums[i % 8] = sums[i % 8] + parts[i]
        total[0] = ((sums[0] + sums[1]) + (sums[2] + sums[3])) + ((sums[4] + sums[5]) + (sums[6] + sums[7]))
        for i in range(3):
            to_served(i).start()

    @pl.when(jnp.logical_not(is_root))
    def _():
        to_served(0).wait_recv()

    cells = count * planes * rows * lanes
    scale = nz * lanes / (DIFFUSIVITY * (HOT_WALL - COLD_WALL)) / cells
    nusselt[0, 0] = 1.0 + scale * jnp.sum(total[0])

    whole(roots - 1, 0).wait_send()

    @pl.when(jnp.logical_not(is_root))
    def _():
        to_root(0, 1).wait_send()

    @pl.when(is_root)
    def _():
        for i in range(3):
            to_served(i).wait_send()

    for s in range(STEPS):
        drain(s, END_PLANES + ALL_PLANES)


def per_device(shape, flow_pops, heat_pops):
    nx, ny, nz = shape
    _, planes, rows, lanes = flow_pops.shape
    flat = (planes * rows, lanes)
    dma = pltpu.SemaphoreType.DMA
    tile = (rows, lanes)
    vmem = lambda *dims: pltpu.VMEM(dims, jnp.float32)
    anywhere = pl.BlockSpec(memory_space=pl.ANY)
    in_vmem = pl.BlockSpec(memory_space=pltpu.VMEM)
    flow, heat, nusselt = pl.pallas_call(
        functools.partial(kernel, shape, (planes, rows, lanes)),
        out_shape=(
            vmem(FLOWS, *flat),
            vmem(7, *flat),
            jax.ShapeDtypeStruct((1, 1), jnp.float32),
        ),
        in_specs=[anywhere] * 2,
        out_specs=(in_vmem, in_vmem, pl.BlockSpec(memory_space=pltpu.SMEM)),
        scratch_shapes=[
            vmem(POPS, *flat),
            vmem(STEPS, POPS, (planes + 2) * rows, lanes),
            vmem(STEPS, 2, FACE, *tile),
            vmem(STEPS, 2, FACE, *tile),
            vmem(STEPS, len(XY), *tile),
            vmem(STEPS, 2, *tile),
            vmem(STEPS, 2, 3, *tile),
            vmem(STEPS, len(XZ), *tile),
            vmem(1, 1, lanes),
            vmem(nx * ny * nz, 1, lanes),
            vmem(1, 1, lanes),
            dma((6,)),
            dma((STEPS, len(MESSAGES))),
            dma((STEPS, len(MESSAGES))),
            dma((2,)),
            dma((1,)),
            dma((3,)),
            dma((1,)),
        ],
        compiler_params=pltpu.CompilerParams(collective_id=0, has_side_effects=True),
        name="lattice_steps",
    )(flow_pops.reshape((FLOWS,) + flat), heat_pops.reshape((7,) + flat))
    return flow.reshape(flow_pops.shape), heat.reshape(heat_pops.shape), nusselt.reshape(())


def solution(mesh):
    shape = tuple(mesh.shape[a] for a in AXES)
    spec = P(None, *AXES)
    return jax.shard_map(
        functools.partial(per_device, shape),
        mesh=mesh,
        in_specs=(spec, spec),
        out_specs=(spec, spec, P()),
        check_vma=False,
    )
```

time: 47.4 us -> 40.8 us (0.86)
  Pallas kernels: 42.2 us -> 36.5 us
  local copies, waits for them, and re-layouts: 2.69 us -> 1.52 us
    pallas_call x1, Pallas kernels: 42.2 us -> 36.5 us  [per_device(): pl.pallas_call(functools.partial(kernel, shape, (planes, rows, lanes)), o...]
    unnamed x4 -> x2, local copies, waits for them, and re-layouts: 2.69 us -> 1.52 us
where the time goes in v2:
time: 40.8 us; the launch traced here: 40.3 us
  Pallas kernels  36.5 us (89%)
  between operations  2.33 us (6%)
  local copies, waits for them, and re-layouts  1.52 us (4%)
    pallas_call x1, Pallas kernels, per_device(): pl.pallas_call(functools.partial(kernel, shape, (planes, rows, lanes)), o...  36.5 us
    unnamed x2, local copies, waits for them, and re-layouts  1.52 us

profile of v2, /device:TPU:1, one launch (start us, length us, event | category | flops | bytes accessed | tf_op | source)
XLA Modules:
  0.0 40.3 jit_solution(15133312930990912346)
XLA Ops:
  0.6 36.5 %lattice_steps.1 = (f32[19,64,128]{2,1,0:T(8,128)S(1)}, f32[7,64,128]{2,1,0:T(8,128)S(1)}, f32[1,1]{1,0:T(1,128)}) custom-call(f32[19,64,128]{2,1,0:T(8,128)} %bitcast.7, f32[7,64,128]{2,1,0:T(8,128)} %bitcast.8), custom_call_target="tpu_custom_call" | custom-call | tf_op jit(solution)/shard_map/lattice_steps/pallas_call | solution.py:477
  37.1 0.8 %copy.8 = f32[19,8,8,128]{3,2,1,0:T(8,128)} copy(f32[19,8,8,128]{3,2,1,0:T(8,128)S(1)} %bitcast.5) | data formatting | bytes 1245184
  38.0 0.7 %copy.9 = f32[7,8,8,128]{3,2,1,0:T(8,128)} copy(f32[7,8,8,128]{3,2,1,0:T(8,128)S(1)} %bitcast.6) | data formatting | bytes 458752

commit v3 on v2

--- a/solution.py
+++ b/solution.py
@@ -211,16 +211,8 @@
 
     @pl.when(is_root)
     def _():
-        def tell(d, carry):
-            pl.semaphore_signal(
-                barrier,
-                inc=1,
-                device_id=lax.rem(my_index + d, count),
-                device_id_type=pl.DeviceIdType.LOGICAL,
-            )
-            return carry
-
-        lax.fori_loop(1, count, tell, 0)
+        for d in range(1, nx):
+            pl.semaphore_signal(barrier, inc=1, device_id=at((d, 0, 0)), device_id_type=MESH)
 
     lane = lax.broadcasted_iota(jnp.int32, (rows, lanes), 1)
     row = lax.broadcasted_iota(jnp.int32, (rows, lanes), 0)
@@ -347,7 +339,7 @@
         c.wait()
     for x in ends:
         first(x, packed)
-    pl.semaphore_wait(barrier, len(offsets) + roots - is_root.astype(jnp.int32))
+    pl.semaphore_wait(barrier, len(offsets) + nx // 4 - is_root.astype(jnp.int32))
     start(0, END_PLANES)
     for c in loads[4:]:
         c.wait()
@@ -463,6 +455,17 @@
 
     for s in range(STEPS):
         drain(s, END_PLANES + ALL_PLANES)
+
+
+def write_out(flow, heat, flow_out, heat_out, sem):
+    copies = [
+        pltpu.make_async_copy(flow, flow_out, sem.at[0]),
+        pltpu.make_async_copy(heat, heat_out, sem.at[1]),
+    ]
+    for c in copies:
+        c.start()
+    for c in copies:
+        c.wait()
 
 
 def per_device(shape, flow_pops, heat_pops):
@@ -506,6 +509,16 @@
         compiler_params=pltpu.CompilerParams(collective_id=0, has_side_effects=True),
         name="lattice_steps",
     )(flow_pops.reshape((FLOWS,) + flat), heat_pops.reshape((7,) + flat))
+    flow = pltpu.with_memory_space_constraint(flow, pltpu.VMEM)
+    heat = pltpu.with_memory_space_constraint(heat, pltpu.VMEM)
+    flow, heat = pl.pallas_call(
+        write_out,
+        out_shape=(jax.ShapeDtypeStruct((FLOWS,) + flat, jnp.float32), jax.ShapeDtypeStruct((7,) + flat, jnp.float32)),
+        in_specs=[in_vmem] * 2,
+        out_specs=(anywhere, anywhere),
+        scratch_shapes=[dma((2,))],
+        name="write_out",
+    )(flow, heat)
     return flow.reshape(flow_pops.shape), heat.reshape(heat_pops.shape), nusselt.reshape(())
 
 

time: 40.8 us -> 39.1 us (0.958)
  local copies, waits for them, and re-layouts: 1.52 us -> 0 us
    unnamed x2 -> x0, local copies, waits for them, and re-layouts: 1.52 us -> none
    pallas_call x1, Pallas kernels: 36.5 us -> 35.3 us  [per_device(): pl.pallas_call(functools.partial(kernel, shape, (planes, rows, lanes)), o...]
    pallas_call x0 -> x1, Pallas kernels: none -> 0.91 us  [per_device(): pl.pallas_call(write_out, out_shape=(jax.ShapeDtypeStruct((FLOWS,) + flat...]
where the time goes in v3:
time: 39.1 us; the launch traced here: 38.6 us
  Pallas kernels  36.2 us (93%)
  between operations  2.4 us (6%)
    pallas_call x1, Pallas kernels, per_device(): pl.pallas_call(functools.partial(kernel, shape, (planes, rows, lanes)), o...  35.3 us
    pallas_call x1, Pallas kernels, per_device(): pl.pallas_call(write_out, out_shape=(jax.ShapeDtypeStruct((FLOWS,) + flat...  0.91 us

profile of v3, /device:TPU:1, one launch (start us, length us, event | category | flops | bytes accessed | tf_op | source)
XLA Modules:
  0.0 38.6 jit_solution(17240354334898844853)
XLA Ops:
  0.6 35.3 %lattice_steps.1 = (f32[19,64,128]{2,1,0:T(8,128)S(1)}, f32[7,64,128]{2,1,0:T(8,128)S(1)}, f32[1,1]{1,0:T(1,128)}) custom-call(f32[19,64,128]{2,1,0:T(8,128)} %bitcast.5, f32[7,64,128]{2,1,0:T(8,128)} %bitcast.6), custom_call_target="tpu_custom_call" | custom-call | tf_op jit(solution)/shard_map/lattice_steps/pallas_call | solution.py:480
  35.9 0.9 %write_out.1 = (f32[19,64,128]{2,1,0:T(8,128)}, f32[7,64,128]{2,1,0:T(8,128)}) custom-call(f32[19,64,128]{2,1,0:T(8,128)S(1)} %get-tuple-element.8.flow, f32[7,64,128]{2,1,0:T(8,128)S(1)} %get-tuple-element.9.heat), custom_call_target="tpu_custom_call" | custom-call | tf_op jit(solution)/shard_map/write_out/pallas_call | solution.py:514

commit v4 on v3

--- a/solution.py
+++ b/solution.py
@@ -68,14 +68,16 @@
     out = [("x", 1, (1, 0, 0)), ("x", -1, (-1, 0, 0))]
     out += [("xz", q, LATTICE[q]) for q in XZ]
     out += [("xy", q, LATTICE[q]) for q in XY]
-    out += [("z", (cz, cy), (0, cy, cz)) for cz in (1, -1) for cy in (1, -1, 0)]
+    out += [("yz", (cz, cy), (0, cy, cz)) for cz in (1, -1) for cy in (1, -1)]
+    out += [("z", cz, (0, 0, cz)) for cz in (1, -1)]
     out += [("y", 1, (0, 1, 0)), ("y", -1, (0, -1, 0))]
     return out
 
 
 MESSAGES = messages()
+EDGE = {m[:2]: i for i, m in enumerate(m for m in MESSAGES if m[0] in ("xy", "yz"))}
 END_PLANES = ("x", "xy", "xz")
-ALL_PLANES = ("y", "z")
+ALL_PLANES = ("y", "z", "yz")
 
 
 def collide(f):
@@ -159,18 +161,18 @@
     heat_in,
     flow_out,
     heat_out,
-    nusselt,
+    total,
     held,
     post,
     ysend,
     yrecv,
-    ydiag,
     zsend,
     zrecv,
     zdiag,
+    edge_send,
+    edge_recv,
     part,
     parts,
-    total,
     in_sem,
     send_sem,
     recv_sem,
@@ -184,9 +186,8 @@
     me = tuple(lax.axis_index(a) for a in AXES)
     count = nx * ny * nz
     group = ny * nz
-    roots = (nx // 4) * group
     my_index = me[0] * group + me[1] * nz + me[2]
-    is_root = me[0] < nx // 4
+    is_root = lax.rem(me[0], nx // 2) < nx // 4
 
     def at(off):
         return tuple(m if d == 0 else lax.rem(m + (d % n), n) for m, d, n in zip(me, off, shape))
@@ -232,6 +233,12 @@
         return pl.ds((x + 1) * rows, rows)
 
     def keep(s, x, out, packed):
+        if x in ends:
+            cx = 1 if x else -1
+            for q in XY:
+                if LATTICE[q][0] == cx:
+                    far = far_row[LATTICE[q][1]]
+                    edge_send[s, EDGE["xy", q]] = out[q][far : far + 1, :]
         for q in range(POPS):
             post[s, POS[q], plane(x), :] = out[q]
         for cz in (1, -1):
@@ -248,11 +255,12 @@
         elif kind == "y":
             src, dst = ysend.at[s, side[slot]], yrecv.at[s, side[slot]]
         elif kind == "z":
-            cz, cy = slot
-            src, dst = zsend.at[s, side[cz]], zrecv.at[s, side[cz], cy + 1]
+            src, dst = zsend.at[s, side[slot]], zrecv.at[s, side[slot]]
+        elif kind == "xz":
+            src = post.at[s, POS[slot], plane(planes - 1 if off[0] == 1 else 0)]
+            dst = zdiag.at[s, XZ.index(slot)]
         else:
-            src = post.at[s, POS[slot], plane(planes - 1 if off[0] == 1 else 0)]
-            dst = ydiag.at[s, XY.index(slot)] if kind == "xy" else zdiag.at[s, XZ.index(slot)]
+            src, dst = edge_send.at[s, EDGE[kind, slot]], edge_recv.at[s, EDGE[kind, slot]]
         return pltpu.make_async_remote_copy(
             src_ref=src,
             dst_ref=dst,
@@ -293,15 +301,18 @@
                 ysend[s, side[cy], j] = post[s, POS[q], pl.ds(first, planes, stride=rows), :]
         for cz in (1, -1):
             zsend[s, side[cz]] = packed[cz]
+            for cy in (1, -1):
+                far = far_row[cy]
+                edge_send[s, EDGE["yz", (cz, cy)]] = packed[cz][far : far + 1, :]
 
     def z_faces(s):
         tiles = {}
         for cz in (1, -1):
-            own = zrecv[s, side[cz], 1]
+            own = zrecv[s, side[cz]]
             tiles[cz, 0] = own
             for cy in (1, -1):
-                other = zrecv[s, side[cz], cy + 1]
-                tiles[cz, cy] = turn(jnp.where(row == far_row[cy], other, own), cy, 0)
+                other = jnp.broadcast_to(edge_recv[s, EDGE["yz", (cz, cy)]], (rows, lanes))
+                tiles[cz, cy] = jnp.where(end_row[cy], other, turn(own, cy, 0))
         return tiles
 
     def stream(s, x, tiles):
@@ -314,7 +325,7 @@
                 if inside:
                     edge = yrecv[s, side[cy], YM[cy].index(q), pl.ds(x - cx, 1), :]
                 else:
-                    edge = ydiag[s, XY.index(q), pl.ds(far_row[cy], 1), :]
+                    edge = edge_recv[s, EDGE["xy", q]]
                 v = jnp.where(end_row[cy], jnp.broadcast_to(edge, (rows, lanes)), turn(v, cy, 0))
             if cz:
                 if inside:
@@ -339,7 +350,7 @@
         c.wait()
     for x in ends:
         first(x, packed)
-    pl.semaphore_wait(barrier, len(offsets) + nx // 4 - is_root.astype(jnp.int32))
+    pl.semaphore_wait(barrier, len(offsets) + nx // 2 - is_root.astype(jnp.int32))
     start(0, END_PLANES)
     for c in loads[4:]:
         c.wait()
@@ -381,27 +392,31 @@
     mine = jnp.sum(acc, axis=0, keepdims=True)
     part[0] = mine
     parts[my_index] = mine
-    base = lax.rem(my_index, roots)
-
-    def to_root(d, k):
+    seat = lax.rem(my_index, group)
+    half = nx // 2
+    lines = [x for x in range(nx) if x % half < nx // 4]
+
+    def to_root(x, d, sem):
         return pltpu.make_async_remote_copy(
             src_ref=part.at[0],
             dst_ref=parts.at[my_index],
-            send_sem=part_send.at[k],
+            send_sem=part_send.at[sem],
             recv_sem=part_recv.at[0],
-            device_id=lax.rem(base + d, roots),
+            device_id=x * group + lax.rem(seat + d, group),
             device_id_type=pl.DeviceIdType.LOGICAL,
         )
 
-    for d in range(1, roots):
-        to_root(d, 0).start()
-
-    @pl.when(jnp.logical_not(is_root))
-    def _():
-        to_root(0, 1).start()
-
-    half = nx // 2
-    served = [me[0] + half, half - 1 - me[0], nx - 1 - me[0]]
+    def not_self(x, act):
+        @pl.when(me[0] != x)
+        def _():
+            act(to_root(x, 0, 1 + lines.index(x)))
+
+    for x in lines:
+        not_self(x, lambda c: c.start())
+        for d in range(1, group):
+            to_root(x, d, 0).start()
+
+    served = [half - 1 - lax.rem(me[0], half) + half * lax.div(me[0], half)]
 
     def to_served(i):
         return pltpu.make_async_remote_copy(
@@ -431,39 +446,34 @@
         for i in range(8, count):
             sums[i % 8] = sums[i % 8] + parts[i]
         total[0] = ((sums[0] + sums[1]) + (sums[2] + sums[3])) + ((sums[4] + sums[5]) + (sums[6] + sums[7]))
-        for i in range(3):
+        for i in range(1):
             to_served(i).start()
 
     @pl.when(jnp.logical_not(is_root))
     def _():
         to_served(0).wait_recv()
 
-    cells = count * planes * rows * lanes
-    scale = nz * lanes / (DIFFUSIVITY * (HOT_WALL - COLD_WALL)) / cells
-    nusselt[0, 0] = 1.0 + scale * jnp.sum(total[0])
-
-    whole(roots - 1, 0).wait_send()
-
-    @pl.when(jnp.logical_not(is_root))
-    def _():
-        to_root(0, 1).wait_send()
+    whole(len(lines) * (group - 1), 0).wait_send()
+    for x in lines:
+        not_self(x, lambda c: c.wait_send())
 
     @pl.when(is_root)
     def _():
-        for i in range(3):
+        for i in range(1):
             to_served(i).wait_send()
 
     for s in range(STEPS):
         drain(s, END_PLANES + ALL_PLANES)
 
 
-def write_out(flow, heat, flow_out, heat_out, sem):
+def write_out(scale, flow, heat, total, flow_out, heat_out, nusselt, sem):
     copies = [
         pltpu.make_async_copy(flow, flow_out, sem.at[0]),
         pltpu.make_async_copy(heat, heat_out, sem.at[1]),
     ]
     for c in copies:
         c.start()
+    nusselt[0, 0] = 1.0 + scale * jnp.sum(total[0])
     for c in copies:
         c.wait()
 
@@ -477,48 +487,52 @@
     vmem = lambda *dims: pltpu.VMEM(dims, jnp.float32)
     anywhere = pl.BlockSpec(memory_space=pl.ANY)
     in_vmem = pl.BlockSpec(memory_space=pltpu.VMEM)
-    flow, heat, nusselt = pl.pallas_call(
+    state = pl.pallas_call(
         functools.partial(kernel, shape, (planes, rows, lanes)),
         out_shape=(
             vmem(FLOWS, *flat),
             vmem(7, *flat),
-            jax.ShapeDtypeStruct((1, 1), jnp.float32),
+            vmem(1, 1, lanes),
         ),
         in_specs=[anywhere] * 2,
-        out_specs=(in_vmem, in_vmem, pl.BlockSpec(memory_space=pltpu.SMEM)),
+        out_specs=(in_vmem,) * 3,
         scratch_shapes=[
             vmem(POPS, *flat),
             vmem(STEPS, POPS, (planes + 2) * rows, lanes),
             vmem(STEPS, 2, FACE, *tile),
             vmem(STEPS, 2, FACE, *tile),
-            vmem(STEPS, len(XY), *tile),
             vmem(STEPS, 2, *tile),
-            vmem(STEPS, 2, 3, *tile),
+            vmem(STEPS, 2, *tile),
             vmem(STEPS, len(XZ), *tile),
+            vmem(STEPS, len(EDGE), 1, lanes),
+            vmem(STEPS, len(EDGE), 1, lanes),
             vmem(1, 1, lanes),
             vmem(nx * ny * nz, 1, lanes),
-            vmem(1, 1, lanes),
             dma((6,)),
             dma((STEPS, len(MESSAGES))),
             dma((STEPS, len(MESSAGES))),
-            dma((2,)),
+            dma((1 + nx // 2,)),
             dma((1,)),
-            dma((3,)),
+            dma((1,)),
             dma((1,)),
         ],
         compiler_params=pltpu.CompilerParams(collective_id=0, has_side_effects=True),
         name="lattice_steps",
     )(flow_pops.reshape((FLOWS,) + flat), heat_pops.reshape((7,) + flat))
-    flow = pltpu.with_memory_space_constraint(flow, pltpu.VMEM)
-    heat = pltpu.with_memory_space_constraint(heat, pltpu.VMEM)
-    flow, heat = pl.pallas_call(
-        write_out,
-        out_shape=(jax.ShapeDtypeStruct((FLOWS,) + flat, jnp.float32), jax.ShapeDtypeStruct((7,) + flat, jnp.float32)),
-        in_specs=[in_vmem] * 2,
-        out_specs=(anywhere, anywhere),
+    cells = nx * ny * nz * planes * rows * lanes
+    scale = nz * lanes / (DIFFUSIVITY * (HOT_WALL - COLD_WALL)) / cells
+    flow, heat, nusselt = pl.pallas_call(
+        functools.partial(write_out, scale),
+        out_shape=(
+            jax.ShapeDtypeStruct((FLOWS,) + flat, jnp.float32),
+            jax.ShapeDtypeStruct((7,) + flat, jnp.float32),
+            jax.ShapeDtypeStruct((1, 1), jnp.float32),
+        ),
+        in_specs=[in_vmem] * 3,
+        out_specs=(anywhere, anywhere, pl.BlockSpec(memory_space=pltpu.SMEM)),
         scratch_shapes=[dma((2,))],
         name="write_out",
-    )(flow, heat)
+    )(*(pltpu.with_memory_space_constraint(a, pltpu.VMEM) for a in state))
     return flow.reshape(flow_pops.shape), heat.reshape(heat_pops.shape), nusselt.reshape(())
 
 

time: 39.1 us -> 36.7 us (0.939); the launches traced: 38.6 us -> 36.6 us
  between operations: 2.4 us -> 0.64 us
    pallas_call x1, Pallas kernels: 35.3 us -> 34.6 us  [per_device(): pl.pallas_call(functools.partial(kernel, shape, (planes, rows, lanes)), o...]
    pallas_call x1, Pallas kernels: 0.91 us -> 1.43 us  [per_device(): pl.pallas_call(functools.partial(write_out, scale), out_shape=(jax.ShapeD...]
where the time goes in v4:
time: 36.7 us; the launch traced here: 36.6 us
  Pallas kernels  36 us (98%)
  between operations  0.64 us (2%)
    pallas_call x1, Pallas kernels, per_device(): pl.pallas_call(functools.partial(kernel, shape, (planes, rows, lanes)), o...  34.6 us
    pallas_call x1, Pallas kernels, per_device(): pl.pallas_call(functools.partial(write_out, scale), out_shape=(jax.ShapeD...  1.43 us

profile of v4, /device:TPU:1, one launch (start us, length us, event | category | flops | bytes accessed | tf_op | source)
XLA Modules:
  0.0 36.6 jit_solution(5847671671257284390)
XLA Ops:
  0.6 34.6 %lattice_steps.1 = (f32[19,64,128]{2,1,0:T(8,128)S(1)}, f32[7,64,128]{2,1,0:T(8,128)S(1)}, f32[1,1,128]{2,1,0:T(1,128)S(1)}) custom-call(f32[19,64,128]{2,1,0:T(8,128)} %bitcast.5, f32[7,64,128]{2,1,0:T(8,128)} %bitcast.6), custom_call_target="tpu_custom_call" | custom-call | tf_op jit(solution)/shard_map/lattice_steps/pallas_call | solution.py:490
  35.2 1.4 %write_out.1 = (f32[19,64,128]{2,1,0:T(8,128)}, f32[7,64,128]{2,1,0:T(8,128)}, f32[1,1]{1,0:T(1,128)}) custom-call(f32[19,64,128]{2,1,0:T(8,128)S(1)} %get-tuple-element.9.flow, f32[7,64,128]{2,1,0:T(8,128)S(1)} %get-tuple-element.10.heat, f32[1,1,128]{2,1,0:T(1,128)S(1)} %get-tuple-element.11.total), custom_call_target="tpu_custom_call" | custom-call | tf_op jit(solution)/shard_map/write_out/pallas_call | solution.py:524

commit v5 on v4

--- a/solution.py
+++ b/solution.py
@@ -246,6 +246,9 @@
                 k = LANE0 + j * planes + x
                 packed[cz] = jnp.where(lane == k, pltpu.roll(out[q], k + (1 if cz == 1 else 0), 1), packed[cz])
 
+    def crew(end, dz):
+        return (0 if end else 3) + dz + 1
+
     def copy(s, m):
         kind, slot, off = MESSAGES[m]
         if kind == "x":
@@ -264,8 +267,8 @@
         return pltpu.make_async_remote_copy(
             src_ref=src,
             dst_ref=dst,
-            send_sem=send_sem.at[s, m],
-            recv_sem=recv_sem.at[s, m],
+            send_sem=send_sem.at[s, crew(kind in END_PLANES, off[2])],
+            recv_sem=recv_sem.at[s, crew(kind in END_PLANES, off[2])],
             device_id=at(off),
             device_id_type=MESH,
         )
@@ -273,26 +276,39 @@
     def of_kind(kinds, dz):
         return [m for m, (kind, _, off) in enumerate(MESSAGES) if kind in kinds and off[2] == dz]
 
-    def each(s, kinds, act, up, down):
+    def each(act, up, down):
         for dz, when in ((1, up), (-1, down)):
-            if of_kind(kinds, dz):
-
-                @pl.when(when)
-                def _():
-                    for m in of_kind(kinds, dz):
-                        act(copy(s, m))
-
-        for m in of_kind(kinds, 0):
-            act(copy(s, m))
+
+            @pl.when(when)
+            def _():
+                act(dz)
+
+        act(0)
 
     def start(s, kinds):
-        each(s, kinds, lambda c: c.start(), jnp.logical_not(is_top), jnp.logical_not(is_bottom))
+        def act(dz):
+            for m in of_kind(kinds, dz):
+                copy(s, m).start()
+
+        each(act, jnp.logical_not(is_top), jnp.logical_not(is_bottom))
+
+    def bytes_of(s, kinds, dz):
+        size = {"x": FACE * rows, "y": FACE * planes, "z": rows, "xz": rows, "xy": 1, "yz": 1}
+        some = parts.at[pl.ds(0, sum(size[MESSAGES[m][0]] for m in of_kind(kinds, dz)))]
+        return pltpu.make_async_remote_copy(
+            src_ref=some,
+            dst_ref=some,
+            send_sem=send_sem.at[s, crew(kinds == END_PLANES, dz)],
+            recv_sem=recv_sem.at[s, crew(kinds == END_PLANES, dz)],
+            device_id=at((1, 0, 0)),
+            device_id_type=MESH,
+        )
 
     def receive(s, kinds):
-        each(s, kinds, lambda c: c.wait_recv(), jnp.logical_not(is_bottom), jnp.logical_not(is_top))
+        each(lambda dz: bytes_of(s, kinds, dz).wait_recv(), jnp.logical_not(is_bottom), jnp.logical_not(is_top))
 
     def drain(s, kinds):
-        each(s, kinds, lambda c: c.wait_send(), jnp.logical_not(is_top), jnp.logical_not(is_bottom))
+        each(lambda dz: bytes_of(s, kinds, dz).wait_send(), jnp.logical_not(is_top), jnp.logical_not(is_bottom))
 
     def pack(s, packed):
         for cy in (1, -1):
@@ -396,25 +412,24 @@
     half = nx // 2
     lines = [x for x in range(nx) if x % half < nx // 4]
 
-    def to_root(x, d, sem):
+    def to_root(x, d):
         return pltpu.make_async_remote_copy(
             src_ref=part.at[0],
             dst_ref=parts.at[my_index],
-            send_sem=part_send.at[sem],
+            send_sem=part_send.at[0],
             recv_sem=part_recv.at[0],
             device_id=x * group + lax.rem(seat + d, group),
             device_id_type=pl.DeviceIdType.LOGICAL,
         )
 
-    def not_self(x, act):
+    for x in lines:
+
         @pl.when(me[0] != x)
         def _():
-            act(to_root(x, 0, 1 + lines.index(x)))
-
-    for x in lines:
-        not_self(x, lambda c: c.start())
+            to_root(x, 0).start()
+
         for d in range(1, group):
-            to_root(x, d, 0).start()
+            to_root(x, d).start()
 
     served = [half - 1 - lax.rem(me[0], half) + half * lax.div(me[0], half)]
 
@@ -439,6 +454,18 @@
             device_id_type=pl.DeviceIdType.LOGICAL,
         )
 
+    for s in range(STEPS):
+        drain(s, END_PLANES)
+        drain(s, ALL_PLANES)
+
+    @pl.when(is_root)
+    def _():
+        whole(len(lines) * group - 1, 0).wait_send()
+
+    @pl.when(jnp.logical_not(is_root))
+    def _():
+        whole(len(lines) * group, 0).wait_send()
+
     @pl.when(is_root)
     def _():
         whole(count - 1, 0).wait_recv()
@@ -453,27 +480,22 @@
     def _():
         to_served(0).wait_recv()
 
-    whole(len(lines) * (group - 1), 0).wait_send()
-    for x in lines:
-        not_self(x, lambda c: c.wait_send())
-
     @pl.when(is_root)
     def _():
         for i in range(1):
             to_served(i).wait_send()
 
-    for s in range(STEPS):
-        drain(s, END_PLANES + ALL_PLANES)
-
-
-def write_out(scale, flow, heat, total, flow_out, heat_out, nusselt, sem):
+
+def write_out(scale, flow, heat, total, flow_out, heat_out, nusselt, value, sem):
     copies = [
         pltpu.make_async_copy(flow, flow_out, sem.at[0]),
         pltpu.make_async_copy(heat, heat_out, sem.at[1]),
     ]
     for c in copies:
         c.start()
-    nusselt[0, 0] = 1.0 + scale * jnp.sum(total[0])
+    value[...] = 1.0 + scale * jnp.sum(total[0], axis=1, keepdims=True)
+    copies.append(pltpu.make_async_copy(value, nusselt, sem.at[2]))
+    copies[2].start()
     for c in copies:
         c.wait()
 
@@ -507,11 +529,11 @@
             vmem(STEPS, len(EDGE), 1, lanes),
             vmem(STEPS, len(EDGE), 1, lanes),
             vmem(1, 1, lanes),
-            vmem(nx * ny * nz, 1, lanes),
+            vmem(max(nx * ny * nz, 128), 1, lanes),
             dma((6,)),
-            dma((STEPS, len(MESSAGES))),
-            dma((STEPS, len(MESSAGES))),
-            dma((1 + nx // 2,)),
+            dma((STEPS, 6)),
+            dma((STEPS, 6)),
+            dma((1,)),
             dma((1,)),
             dma((1,)),
             dma((1,)),
@@ -529,8 +551,8 @@
             jax.ShapeDtypeStruct((1, 1), jnp.float32),
         ),
         in_specs=[in_vmem] * 3,
-        out_specs=(anywhere, anywhere, pl.BlockSpec(memory_space=pltpu.SMEM)),
-        scratch_shapes=[dma((2,))],
+        out_specs=(anywhere,) * 3,
+        scratch_shapes=[vmem(1, 1), dma((3,))],
         name="write_out",
     )(*(pltpu.with_memory_space_constraint(a, pltpu.VMEM) for a in state))
     return flow.reshape(flow_pops.shape), heat.reshape(heat_pops.shape), nusselt.reshape(())

time: 36.7 us -> 35.4 us (0.965)
  Pallas kernels: 36 us -> 34.7 us
    pallas_call x1, Pallas kernels: 34.6 us -> 33.8 us  [per_device(): pl.pallas_call(functools.partial(kernel, shape, (planes, rows, lanes)), o...]
    pallas_call x1, Pallas kernels: 1.43 us -> 0.92 us  [per_device(): pl.pallas_call(functools.partial(write_out, scale), out_shape=(jax.ShapeD...]
where the time goes in v5:
time: 35.4 us; the launch traced here: 35.3 us
  Pallas kernels  34.7 us (98%)
  between operations  0.64 us (2%)
    pallas_call x1, Pallas kernels, per_device(): pl.pallas_call(functools.partial(kernel, shape, (planes, rows, lanes)), o...  33.8 us
    pallas_call x1, Pallas kernels, per_device(): pl.pallas_call(functools.partial(write_out, scale), out_shape=(jax.ShapeD...  0.92 us

profile of v5, /device:TPU:1, one launch (start us, length us, event | category | flops | bytes accessed | tf_op | source)
XLA Modules:
  0.0 35.3 jit_solution(18006106163561360203)
XLA Ops:
  0.6 33.8 %lattice_steps.1 = (f32[19,64,128]{2,1,0:T(8,128)S(1)}, f32[7,64,128]{2,1,0:T(8,128)S(1)}, f32[1,1,128]{2,1,0:T(1,128)S(1)}) custom-call(f32[19,64,128]{2,1,0:T(8,128)} %bitcast.5, f32[7,64,128]{2,1,0:T(8,128)} %bitcast.6), custom_call_target="tpu_custom_call" | custom-call | tf_op jit(solution)/shard_map/lattice_steps/pallas_call | solution.py:512
  34.4 0.9 %write_out.1 = (f32[19,64,128]{2,1,0:T(8,128)}, f32[7,64,128]{2,1,0:T(8,128)}, f32[1,1]{1,0:T(1,128)}) custom-call(f32[19,64,128]{2,1,0:T(8,128)S(1)} %get-tuple-element.9.flow, f32[7,64,128]{2,1,0:T(8,128)S(1)} %get-tuple-element.10.heat, f32[1,1,128]{2,1,0:T(1,128)S(1)} %get-tuple-element.11.total), custom_call_target="tpu_custom_call" | custom-call | tf_op jit(solution)/shard_map/write_out/pallas_call | solution.py:546

commit v6 on v5

--- a/solution.py
+++ b/solution.py
@@ -186,14 +186,16 @@
     me = tuple(lax.axis_index(a) for a in AXES)
     count = nx * ny * nz
     group = ny * nz
+    lines = nx - nx // 4
     my_index = me[0] * group + me[1] * nz + me[2]
-    is_root = lax.rem(me[0], nx // 2) < nx // 4
+    is_root = me[0] < lines
 
     def at(off):
         return tuple(m if d == 0 else lax.rem(m + (d % n), n) for m, d, n in zip(me, off, shape))
 
     offsets = [off for off in np.ndindex(3, 3, 3) if off != (1, 1, 1)]
     offsets = [tuple(d - 1 for d in off) for off in offsets if 1 in off]
+    offsets.sort(key=lambda off: -2 * abs(off[0]) - abs(off[2]))
     barrier = pltpu.get_barrier_semaphore()
     for off in offsets:
         pl.semaphore_signal(barrier, inc=1, device_id=at(off), device_id_type=MESH)
@@ -366,7 +368,7 @@
         c.wait()
     for x in ends:
         first(x, packed)
-    pl.semaphore_wait(barrier, len(offsets) + nx // 2 - is_root.astype(jnp.int32))
+    pl.semaphore_wait(barrier, len(offsets) + lines - is_root.astype(jnp.int32))
     start(0, END_PLANES)
     for c in loads[4:]:
         c.wait()
@@ -409,8 +411,6 @@
     part[0] = mine
     parts[my_index] = mine
     seat = lax.rem(my_index, group)
-    half = nx // 2
-    lines = [x for x in range(nx) if x % half < nx // 4]
 
     def to_root(x, d):
         return pltpu.make_async_remote_copy(
@@ -422,7 +422,7 @@
             device_id_type=pl.DeviceIdType.LOGICAL,
         )
 
-    for x in lines:
+    for x in range(lines):
 
         @pl.when(me[0] != x)
         def _():
@@ -431,7 +431,8 @@
         for d in range(1, group):
             to_root(x, d).start()
 
-    served = [half - 1 - lax.rem(me[0], half) + half * lax.div(me[0], half)]
+    serves = jnp.logical_and(me[0] >= nx // 2, is_root)
+    served = [nx + nx // 2 - 1 - me[0]]
 
     def to_served(i):
         return pltpu.make_async_remote_copy(
@@ -460,11 +461,11 @@
 
     @pl.when(is_root)
     def _():
-        whole(len(lines) * group - 1, 0).wait_send()
+        whole(lines * group - 1, 0).wait_send()
 
     @pl.when(jnp.logical_not(is_root))
     def _():
-        whole(len(lines) * group, 0).wait_send()
+        whole(lines * group, 0).wait_send()
 
     @pl.when(is_root)
     def _():
@@ -473,17 +474,18 @@
         for i in range(8, count):
             sums[i % 8] = sums[i % 8] + parts[i]
         total[0] = ((sums[0] + sums[1]) + (sums[2] + sums[3])) + ((sums[4] + sums[5]) + (sums[6] + sums[7]))
-        for i in range(1):
-            to_served(i).start()
+
+        @pl.when(serves)
+        def _():
+            to_served(0).start()
 
     @pl.when(jnp.logical_not(is_root))
     def _():
         to_served(0).wait_recv()
 
-    @pl.when(is_root)
+    @pl.when(serves)
     def _():
-        for i in range(1):
-            to_served(i).wait_send()
+        to_served(0).wait_send()
 
 
 def write_out(scale, flow, heat, total, flow_out, heat_out, nusselt, value, sem):

time: 35.4 us -> 34.7 us (0.980)
  Pallas kernels: 34.7 us -> 33.9 us
    pallas_call x1, Pallas kernels: 33.8 us -> 32.9 us  [per_device(): pl.pallas_call(functools.partial(kernel, shape, (planes, rows, lanes)), o...]
where the time goes in v6:
time: 34.7 us; the launch traced here: 34.5 us
  Pallas kernels  33.9 us (98%)
  between operations  0.64 us (2%)
    pallas_call x1, Pallas kernels, per_device(): pl.pallas_call(functools.partial(kernel, shape, (planes, rows, lanes)), o...  32.9 us
    pallas_call x1, Pallas kernels, per_device(): pl.pallas_call(functools.partial(write_out, scale), out_shape=(jax.ShapeD...  0.92 us

profile of v6, /device:TPU:1, one launch (start us, length us, event | category | flops | bytes accessed | tf_op | source)
XLA Modules:
  0.0 34.5 jit_solution(13990405120267687999)
XLA Ops:
  0.6 32.9 %lattice_steps.1 = (f32[19,64,128]{2,1,0:T(8,128)S(1)}, f32[7,64,128]{2,1,0:T(8,128)S(1)}, f32[1,1,128]{2,1,0:T(1,128)S(1)}) custom-call(f32[19,64,128]{2,1,0:T(8,128)} %bitcast.5, f32[7,64,128]{2,1,0:T(8,128)} %bitcast.6), custom_call_target="tpu_custom_call" | custom-call | tf_op jit(solution)/shard_map/lattice_steps/pallas_call | solution.py:514
  33.6 0.9 %write_out.1 = (f32[19,64,128]{2,1,0:T(8,128)}, f32[7,64,128]{2,1,0:T(8,128)}, f32[1,1]{1,0:T(1,128)}) custom-call(f32[19,64,128]{2,1,0:T(8,128)S(1)} %get-tuple-element.9.flow, f32[7,64,128]{2,1,0:T(8,128)S(1)} %get-tuple-element.10.heat, f32[1,1,128]{2,1,0:T(1,128)S(1)} %get-tuple-element.11.total), custom_call_target="tpu_custom_call" | custom-call | tf_op jit(solution)/shard_map/write_out/pallas_call | solution.py:548

commit v7 on v6

--- a/solution.py
+++ b/solution.py
@@ -65,9 +65,9 @@
 
 
 def messages():
-    out = [("x", 1, (1, 0, 0)), ("x", -1, (-1, 0, 0))]
-    out += [("xz", q, LATTICE[q]) for q in XZ]
+    out = [("xz", q, LATTICE[q]) for q in XZ]
     out += [("xy", q, LATTICE[q]) for q in XY]
+    out += [("x", 1, (1, 0, 0)), ("x", -1, (-1, 0, 0))]
     out += [("yz", (cz, cy), (0, cy, cz)) for cz in (1, -1) for cy in (1, -1)]
     out += [("z", cz, (0, 0, cz)) for cz in (1, -1)]
     out += [("y", 1, (0, 1, 0)), ("y", -1, (0, -1, 0))]

time: 34.7 us -> 34.7 us (level)
  no operation moved by 1% of the time
where the time goes in v7:
time: 34.7 us; the launch traced here: 34.5 us
  Pallas kernels  33.9 us (98%)
  between operations  0.64 us (2%)
    pallas_call x1, Pallas kernels, per_device(): pl.pallas_call(functools.partial(kernel, shape, (planes, rows, lanes)), o...  32.9 us
    pallas_call x1, Pallas kernels, per_device(): pl.pallas_call(functools.partial(write_out, scale), out_shape=(jax.ShapeD...  0.92 us

profile of v7, /device:TPU:1, one launch (start us, length us, event | category | flops | bytes accessed | tf_op | source)
XLA Modules:
  0.0 34.5 jit_solution(18347529880003874552)
XLA Ops:
  0.6 32.9 %lattice_steps.1 = (f32[19,64,128]{2,1,0:T(8,128)S(1)}, f32[7,64,128]{2,1,0:T(8,128)S(1)}, f32[1,1,128]{2,1,0:T(1,128)S(1)}) custom-call(f32[19,64,128]{2,1,0:T(8,128)} %bitcast.5, f32[7,64,128]{2,1,0:T(8,128)} %bitcast.6), custom_call_target="tpu_custom_call" | custom-call | tf_op jit(solution)/shard_map/lattice_steps/pallas_call | solution.py:514
  33.6 0.9 %write_out.1 = (f32[19,64,128]{2,1,0:T(8,128)}, f32[7,64,128]{2,1,0:T(8,128)}, f32[1,1]{1,0:T(1,128)}) custom-call(f32[19,64,128]{2,1,0:T(8,128)S(1)} %get-tuple-element.9.flow, f32[7,64,128]{2,1,0:T(8,128)S(1)} %get-tuple-element.10.heat, f32[1,1,128]{2,1,0:T(1,128)S(1)} %get-tuple-element.11.total), custom_call_target="tpu_custom_call" | custom-call | tf_op jit(solution)/shard_map/write_out/pallas_call | solution.py:548

commit v8 on v7

--- a/solution.py
+++ b/solution.py
@@ -368,13 +368,13 @@
         c.wait()
     for x in ends:
         first(x, packed)
-    pl.semaphore_wait(barrier, len(offsets) + lines - is_root.astype(jnp.int32))
-    start(0, END_PLANES)
     for c in loads[4:]:
         c.wait()
     for x in inner:
         first(x, packed)
     pack(0, packed)
+    pl.semaphore_wait(barrier, len(offsets) + lines - is_root.astype(jnp.int32))
+    start(0, END_PLANES)
     start(0, ALL_PLANES)
 
     for s in range(1, STEPS):

time: 34.7 us -> 34.7 us (level)
  no operation moved by 1% of the time
where the time goes in v8:
time: 34.7 us; the launch traced here: 34.5 us
  Pallas kernels  33.9 us (98%)
  between operations  0.64 us (2%)
    pallas_call x1, Pallas kernels, per_device(): pl.pallas_call(functools.partial(kernel, shape, (planes, rows, lanes)), o...  33 us
    pallas_call x1, Pallas kernels, per_device(): pl.pallas_call(functools.partial(write_out, scale), out_shape=(jax.ShapeD...  0.92 us

profile of v8, /device:TPU:1, one launch (start us, length us, event | category | flops | bytes accessed | tf_op | source)
XLA Modules:
  0.0 34.5 jit_solution(13889480770720800893)
XLA Ops:
  0.6 33.0 %lattice_steps.1 = (f32[19,64,128]{2,1,0:T(8,128)S(1)}, f32[7,64,128]{2,1,0:T(8,128)S(1)}, f32[1,1,128]{2,1,0:T(1,128)S(1)}) custom-call(f32[19,64,128]{2,1,0:T(8,128)} %bitcast.5, f32[7,64,128]{2,1,0:T(8,128)} %bitcast.6), custom_call_target="tpu_custom_call" | custom-call | tf_op jit(solution)/shard_map/lattice_steps/pallas_call | solution.py:514
  33.6 0.9 %write_out.1 = (f32[19,64,128]{2,1,0:T(8,128)}, f32[7,64,128]{2,1,0:T(8,128)}, f32[1,1]{1,0:T(1,128)}) custom-call(f32[19,64,128]{2,1,0:T(8,128)S(1)} %get-tuple-element.9.flow, f32[7,64,128]{2,1,0:T(8,128)S(1)} %get-tuple-element.10.heat, f32[1,1,128]{2,1,0:T(1,128)S(1)} %get-tuple-element.11.total), custom_call_target="tpu_custom_call" | custom-call | tf_op jit(solution)/shard_map/write_out/pallas_call | solution.py:548

commit v9 on v7

--- a/solution.py
+++ b/solution.py
@@ -212,9 +212,12 @@
     for c in loads:
         c.start()
 
+    far = range(STEPS + 2, nx - STEPS - 1)
+    greeters = sum((lax.rem(me[0] + nx - d, nx) < lines).astype(jnp.int32) for d in far)
+
     @pl.when(is_root)
     def _():
-        for d in range(1, nx):
+        for d in far:
             pl.semaphore_signal(barrier, inc=1, device_id=at((d, 0, 0)), device_id_type=MESH)
 
     lane = lax.broadcasted_iota(jnp.int32, (rows, lanes), 1)
@@ -368,7 +371,7 @@
         c.wait()
     for x in ends:
         first(x, packed)
-    pl.semaphore_wait(barrier, len(offsets) + lines - is_root.astype(jnp.int32))
+    pl.semaphore_wait(barrier, len(offsets) + greeters)
     start(0, END_PLANES)
     for c in loads[4:]:
         c.wait()

time: 34.7 us -> 34.6 us (level)
  no operation moved by 1% of the time
where the time goes in v9:
time: 34.6 us; the launch traced here: 34.5 us
  Pallas kernels  33.9 us (98%)
  between operations  0.64 us (2%)
    pallas_call x1, Pallas kernels, per_device(): pl.pallas_call(functools.partial(kernel, shape, (planes, rows, lanes)), o...  33 us
    pallas_call x1, Pallas kernels, per_device(): pl.pallas_call(functools.partial(write_out, scale), out_shape=(jax.ShapeD...  0.92 us

profile of v9, /device:TPU:1, one launch (start us, length us, event | category | flops | bytes accessed | tf_op | source)
XLA Modules:
  0.0 34.5 jit_solution(4668600595185744043)
XLA Ops:
  0.6 33.0 %lattice_steps.1 = (f32[19,64,128]{2,1,0:T(8,128)S(1)}, f32[7,64,128]{2,1,0:T(8,128)S(1)}, f32[1,1,128]{2,1,0:T(1,128)S(1)}) custom-call(f32[19,64,128]{2,1,0:T(8,128)} %bitcast.5, f32[7,64,128]{2,1,0:T(8,128)} %bitcast.6), custom_call_target="tpu_custom_call" | custom-call | tf_op jit(solution)/shard_map/lattice_steps/pallas_call | solution.py:517
  33.6 0.9 %write_out.1 = (f32[19,64,128]{2,1,0:T(8,128)}, f32[7,64,128]{2,1,0:T(8,128)}, f32[1,1]{1,0:T(1,128)}) custom-call(f32[19,64,128]{2,1,0:T(8,128)S(1)} %get-tuple-element.9.flow, f32[7,64,128]{2,1,0:T(8,128)S(1)} %get-tuple-element.10.heat, f32[1,1,128]{2,1,0:T(1,128)S(1)} %get-tuple-element.11.total), custom_call_target="tpu_custom_call" | custom-call | tf_op jit(solution)/shard_map/write_out/pallas_call | solution.py:551
